TPU v7x, 32 devices: a whole 2x2x4 slice. The times are simulated.
32 devices in a mesh: kpt: 2 (over x), px: 16 (over z, y, core).
Axes of the slice: x: 2, y: 2, z: 4, core: 2. Of those that a mesh axis runs over, the one named last changes fastest.
Arguments:
- right_side: float32 [2, 3, 2, 64, 4096], P(None, None, 'kpt', 'px'), parts along dimension 2, may hold values from -6 to 6
- material: int32 [64, 4096], P('px'), may hold values from 0 to 2
- permittivity: float32 [3], replicated, may hold values from 1 to 2
- bloch_phase: float32 [6], P('kpt'), parts along dimension 0, may hold values from -3.140625 to 3.140625
- quad_shift: float32 [2], replicated, may hold values from 0.05 to 0.6, as said below
Outputs:
- solution: float32 [2, 3, 2, 64, 4096], P(None, None, 'kpt', 'px'), parts along dimension 2
- residual: float32 [2, 3, 2, 64, 4096], P(None, None, 'kpt', 'px'), parts along dimension 2
There are 2 independent parts, one for each index of `kpt`. A program takes and returns all parts, laid end to end along the dimension named above; an argument that names none is the same for every part. Nothing has to cross between parts.
Inputs may be any that keep to these rules, and one draw needn't show every extreme that they name: quad_shift[0] lies in 0.05 to 0.1 and quad_shift[1] in 0.3 to 0.6.
All inputs are finite; a program needn't handle non-finite values.
Results may differ from a plain program's by a relative error of at most 0.0003.
Values sent between devices are 32-bit elements; how exact they have to be, the bound alone decides.
A program may use at most 128 MiB of HBM per device.

v0:
```python
import math

import jax
import jax.numpy as jnp
from jax import lax
from jax.sharding import PartitionSpec as P

NG = 64
ITERS = 3


PRECISE = lax.Precision.HIGHEST


def from_behind(value, axis, steps):
    count = lax.axis_size(axis)
    pairs = [(source, (source + steps) % count) for source in range(count)]
    return lax.ppermute(value, axis, pairs)


def padded(shard, sides, width):
    for axis, dim in sides:
        size, length = (lax.axis_size(axis), shard.shape[dim])
        up = [(i, (i + 1) % size) for i in range(size)]
        down = [(j, i) for i, j in up]
        last = lax.slice_in_dim(shard, length - width, length, axis=dim)
        first = lax.slice_in_dim(shard, 0, width, axis=dim)
        before = lax.ppermute(last, axis, up)
        after = lax.ppermute(first, axis, down)
        shard = jnp.concatenate([before, shard, after], axis=dim)
    return shard


def block_solve(matrix_re, matrix_im, right_re, right_im):
    blocks = matrix_re.shape[0]
    system = jnp.concatenate(
        [jnp.concatenate([matrix_re, -matrix_im], 1), jnp.concatenate([matrix_im, matrix_re], 1)], 0
    )
    values = jnp.concatenate([right_re, right_im], 0)
    doubled = 2 * blocks
    pivot_row = 0
    factors = system[pivot_row + 1 :, pivot_row : pivot_row + 1] / system[pivot_row, pivot_row]
    system = jnp.concatenate(
        [
            system[: pivot_row + 1],
            system[pivot_row + 1 :] - factors * system[pivot_row : pivot_row + 1],
        ],
        0,
    )
    values = jnp.concatenate(
        [
            values[: pivot_row + 1],
            values[pivot_row + 1 :] - factors * values[pivot_row : pivot_row + 1],
        ],
        0,
    )
    rows_out = [None] * doubled
    for pivot_row in range(doubled - 1, -1, -1):
        running = values[pivot_row]
        for later_row in range(pivot_row + 1, doubled):
            running = running - system[pivot_row, later_row] * rows_out[later_row]
        rows_out[pivot_row] = running / system[pivot_row, pivot_row]
    solved = jnp.stack(rows_out, 0)
    return (solved[:blocks], solved[blocks:])


def material_scale(material, permittivity):
    scaled = jnp.zeros(material.shape, jnp.float32)
    for material_id in range(permittivity.shape[0]):
        scaled = scaled + jnp.where(
            material == material_id, permittivity[material_id], jnp.float32(0.0)
        )
    return scaled


def rotate(fields, cosine, sine_part):
    return jnp.stack(
        [cosine * fields[0] - sine_part * fields[1], sine_part * fields[0] + cosine * fields[1]]
    )


def edge_mask(fields, along, target):
    layout = tuple(
        (fields.shape[place_dim] if place_dim == along else 1 for place_dim in range(fields.ndim))
    )
    return lax.broadcasted_iota(jnp.int32, layout, along) == target


def forward_step(fields, along, cosine, sine_part):
    rolled = jnp.roll(fields, -1, along)
    return (
        jnp.where(
            edge_mask(fields, along, fields.shape[along] - 1),
            rotate(rolled, cosine, sine_part),
            rolled,
        )
        - fields
    )


def backward_step(fields, along, cosine, sine_part):
    rolled = jnp.roll(fields, 1, along)
    return (
        jnp.where(edge_mask(fields, along, 0), rotate(rolled, cosine, -sine_part), rolled) - fields
    )


def next_step(fields, upper_next):
    return jnp.concatenate([fields[:, :, 1:], upper_next], 2) - fields


def prior_step(fields, lower_prev):
    return jnp.concatenate([lower_prev, fields[:, :, :-1]], 2) - fields


def curl(fields, upper_next, turn_values):
    cosine_y, sine_y, cosine_z, sine_z = turn_values
    first = forward_step(fields[:, 2], 3, cosine_y, sine_y) - forward_step(
        fields[:, 1], 4, cosine_z, sine_z
    )
    second = forward_step(fields[:, 0], 4, cosine_z, sine_z) - next_step(
        fields[:, 2], upper_next[:, 1]
    )
    third = next_step(fields[:, 1], upper_next[:, 0]) - forward_step(
        fields[:, 0], 3, cosine_y, sine_y
    )
    return jnp.stack([first, second, third], 1)


def curl_adjoint(fields, lower_prev, turn_values):
    cosine_y, sine_y, cosine_z, sine_z = turn_values
    first = backward_step(fields[:, 1], 4, cosine_z, sine_z) - backward_step(
        fields[:, 2], 3, cosine_y, sine_y
    )
    second = prior_step(fields[:, 2], lower_prev[:, 1]) - backward_step(
        fields[:, 0], 4, cosine_z, sine_z
    )
    third = backward_step(fields[:, 0], 3, cosine_y, sine_y) - prior_step(
        fields[:, 1], lower_prev[:, 0]
    )
    return jnp.stack([first, second, third], 1)


def transform_table(theta_value, forward):
    row_index = lax.broadcasted_iota(jnp.int32, (NG, NG), 0)
    col_index = lax.broadcasted_iota(jnp.int32, (NG, NG), 1)
    angles = (
        2.0 * math.pi * (row_index * col_index % NG).astype(jnp.float32) / NG
        + theta_value * col_index.astype(jnp.float32) / NG
    )
    if forward:
        return (jnp.cos(angles), -jnp.sin(angles))
    return (jnp.cos(angles) / NG, jnp.sin(angles) / NG)


def contract(fields, tables, pattern):
    real_part = jnp.einsum(pattern, fields[0], tables[0], precision=PRECISE) - jnp.einsum(
        pattern, fields[1], tables[1], precision=PRECISE
    )
    imag_part = jnp.einsum(pattern, fields[0], tables[1], precision=PRECISE) + jnp.einsum(
        pattern, fields[1], tables[0], precision=PRECISE
    )
    return jnp.stack([real_part, imag_part])


def column_symbol(fields, bloch_phase, damping, col_start):
    length_axis = fields.shape[4]
    mode_index = lax.broadcasted_iota(jnp.int32, (NG, 1), 0).astype(jnp.float32)
    columns = col_start + lax.broadcasted_iota(jnp.int32, (1, length_axis), 1)
    kappa_x = (2.0 * math.pi * mode_index + bloch_phase[0]) / NG
    kappa_y = (2.0 * math.pi * (columns // NG).astype(jnp.float32) + bloch_phase[1]) / NG
    kappa_z = (2.0 * math.pi * (columns % NG).astype(jnp.float32) + bloch_phase[2]) / NG
    differences = [(jnp.cos(kappa) - 1.0, jnp.sin(kappa)) for kappa in (kappa_x, kappa_y, kappa_z)]
    inner_re = sum(
        (
            differences[which_one][0] * fields[0, which_one]
            + differences[which_one][1] * fields[1, which_one]
            for which_one in range(3)
        )
    )
    inner_im = sum(
        (
            differences[which_one][0] * fields[1, which_one]
            - differences[which_one][1] * fields[0, which_one]
            for which_one in range(3)
        )
    )
    magnitude = sum(
        (differences[which_one][0] ** 2 + differences[which_one][1] ** 2 for which_one in range(3))
    )
    outputs = []
    for which_one in range(3):
        diff_re, diff_im = differences[which_one]
        out_re = (fields[0, which_one] + (diff_re * inner_re - diff_im * inner_im) / damping) / (
            magnitude + damping
        )
        out_im = (fields[1, which_one] + (diff_re * inner_im + diff_im * inner_re) / damping) / (
            magnitude + damping
        )
        outputs.append(jnp.stack([out_re, out_im]))
    return jnp.stack(outputs, 1)


def gram(left_side, right_part):
    pattern = "cvxn,cwxn->vw"
    real_part = jnp.einsum(pattern, left_side[0], right_part[0], precision=PRECISE) + jnp.einsum(
        pattern, left_side[1], right_part[1], precision=PRECISE
    )
    imag_part = jnp.einsum(pattern, left_side[0], right_part[1], precision=PRECISE) - jnp.einsum(
        pattern, left_side[1], right_part[0], precision=PRECISE
    )
    return (real_part, imag_part)


def mix(fields, step_coef):
    pattern = "cvxn,vw->cwxn"
    real_part = jnp.einsum(pattern, fields[0], step_coef[0], precision=PRECISE) - jnp.einsum(
        pattern, fields[1], step_coef[1], precision=PRECISE
    )
    imag_part = jnp.einsum(pattern, fields[0], step_coef[1], precision=PRECISE) + jnp.einsum(
        pattern, fields[1], step_coef[0], precision=PRECISE
    )
    return jnp.stack([real_part, imag_part])


def on_device(right_side, material, permittivity, bloch_phase, quad_shift):
    vectors = right_side.shape[2]
    planes = right_side.shape[3]
    position = lax.axis_index("px")
    last_device = lax.axis_size("px") - 1
    permit = material_scale(material, permittivity).reshape(planes, NG, NG)
    inverse_eps = 1.0 / permit
    lower_kind = from_behind(material[-1:], "px", 1)
    inverse_lower = 1.0 / material_scale(lower_kind, permittivity).reshape(1, NG, NG)
    damping = quad_shift[0] * jnp.mean(permittivity)
    turn_values = (
        jnp.cos(bloch_phase[1]),
        jnp.sin(bloch_phase[1]),
        jnp.cos(bloch_phase[2]),
        jnp.sin(bloch_phase[2]),
    )
    is_top = position == last_device
    is_bottom = position == 0
    cosine_up = jnp.where(is_top, jnp.cos(bloch_phase[0]), 1.0)
    sine_up = jnp.where(is_top, jnp.sin(bloch_phase[0]), 0.0)
    cosine_down = jnp.where(is_bottom, jnp.cos(bloch_phase[0]), 1.0)
    sine_down = jnp.where(is_bottom, -jnp.sin(bloch_phase[0]), 0.0)
    forward_tables = [transform_table(bloch_phase[which_one], True) for which_one in range(3)]
    inverse_tables = [transform_table(bloch_phase[which_one], False) for which_one in range(3)]
    columns = NG * NG // lax.axis_size("px")
    col_start = position * columns

    def column_work(pieces):
        spectrum = contract(pieces, forward_tables[0], "cvjn,mj->cvmn")
        spectrum = column_symbol(spectrum, bloch_phase, damping, col_start)
        return contract(spectrum, inverse_tables[0], "cvmn,mj->cvjn")

    def precondition(flat_field):
        fields = flat_field.reshape(2, 3, vectors, planes, NG, NG)
        fields = contract(fields, forward_tables[2], "cvxyj,mj->cvxym")
        fields = contract(fields, forward_tables[1], "cvxjz,mj->cvxmz")
        flat_spectrum = fields.reshape(2, 3, vectors, planes, NG * NG)
        gathered = lax.all_to_all(flat_spectrum, "px", split_axis=4, concat_axis=3, tiled=True)
        worked = column_work(gathered)
        returned = lax.all_to_all(worked, "px", split_axis=3, concat_axis=4, tiled=True)
        fields = returned.reshape(2, 3, vectors, planes, NG, NG)
        fields = contract(fields, inverse_tables[1], "cvxmz,mj->cvxjz")
        fields = contract(fields, inverse_tables[2], "cvxym,mj->cvxyj")
        return fields.reshape(flat_field.shape)

    solution = jnp.zeros_like(right_side)
    residual = right_side
    direction = precondition(residual)
    for iteration in range(ITERS):
        operate_fields = direction.reshape(2, 3, direction.shape[2], planes, NG, NG)
        extended = padded(operate_fields, (("px", 3),), 1)
        bottom = rotate(extended[:, :, :, :1], cosine_down, sine_down)
        top_plane = rotate(extended[:, :, :, -1:], cosine_up, sine_up)
        extended = jnp.concatenate([bottom, extended[:, :, :, 1:-1], top_plane], 3)
        curled = curl(
            extended[:, :, :, :-1], extended[:, 1:3, :, -1:], turn_values
        ) * jnp.concatenate([inverse_lower, inverse_eps], 0)
        result = curl_adjoint(curled[:, :, :, 1:], curled[:, 1:3, :, :1], turn_values)
        mass_term = rotate(operate_fields, quad_shift[0], quad_shift[1]) * permit
        image_dir = (result + mass_term).reshape(direction.shape)
        first_pair = gram(direction, image_dir)
        second_pair = gram(direction, residual)
        totals = lax.psum((first_pair[0], first_pair[1], second_pair[0], second_pair[1]), "px")
        step_coef = block_solve(totals[0], totals[1], totals[2], totals[3])
        solution = solution + mix(direction, step_coef)
        residual = residual - mix(image_dir, step_coef)
        if iteration < ITERS - 1:
            precond = precondition(residual)
            update_pair = gram(image_dir, precond)
            update_totals = lax.psum((update_pair[0], update_pair[1]), "px")
            beta_re, beta_im = block_solve(totals[0], totals[1], update_totals[0], update_totals[1])
            direction = precond + mix(direction, (-beta_re, -beta_im))
    return (solution, residual)


def solution(mesh):
    return jax.shard_map(
        on_device,
        mesh=mesh,
        in_specs=(P(None, None, "kpt", "px", None), P("px", None), P(), P("kpt"), P()),
        out_specs=(P(None, None, "kpt", "px", None), P(None, None, "kpt", "px", None)),
        check_vma=False,
    )
```

profile of v0, /device:TPU:0, one launch (start us, length us, event | category | flops | bytes accessed | tf_op | source)
XLA Modules:
  0.0 819.2 jit_solution(17893291572140384924)
XLA Ops:
  17.2 10.4 %copy.2218 = f32[1,3,1,4,4096]{3,0,2,1,4:T(1,128)} copy(f32[1,3,1,4,4096]{4,3,1,2,0:T(4,128)S(1)} %stack.595) | data formatting | bytes 393216 | tf_op jit(solution)/shard_map/stack | solution.py:163
  27.6 10.1 %copy.2219 = f32[1,3,1,4,4096]{3,0,2,1,4:T(1,128)} copy(f32[1,3,1,4,4096]{4,3,1,2,0:T(4,128)S(1)} %stack.596) | data formatting | bytes 393216 | tf_op jit(solution)/shard_map/stack | solution.py:163
  37.7 16.6 %fusion.762 = f32[4096,3,1,2,4]{4,3,2,1,0:T(2,128)} fusion(f32[1,3,1,4,4096]{3,0,2,1,4:T(1,128)} %copy.2219, f32[1,3,1,4,4096]{3,0,2,1,4:T(1,128)} %copy.2218), kind=kLoop, calls=%fused_computation.1223 | loop fusion | flops 98304 | bytes 786432
  54.4 17.6 %reshape.14430 = f32[16,1,6144]{2,1,0:T(1,128)} reshape(f32[4096,3,1,2,4]{4,3,2,1,0:T(2,128)} %fusion.762) | data formatting | bytes 786432
  72.0 7.2 all-to-all-start
  86.4 5.0 all-to-all-done
  93.4 24.8 %reshape.14431 = f32[4096,3,1,2,4]{4,3,2,1,0:T(2,128)} reshape(f32[16,6144]{1,0:T(8,128)S(1)} %reduce.68) | data formatting | bytes 786432
  118.2 15.5 %copy.2220 = f32[2,3,1,4,16,256]{5,3,4,1,2,0:T(4,128)S(1)} copy(f32[2,3,1,4,16,256]{3,0,1,5,4,2:T(2,128)} %bitcast.1769) | data formatting | bytes 786432 | tf_op jit(solution)/shard_map/all_to_all | solution.py:263
  139.3 4.0 all-to-all-start.1
  143.3 1.9 select_add_fusion
  150.2 2.0 fusion.340
  152.4 3.0 all-to-all-done.1
  162.6 2.2 subtract_bitcast_fusion
  166.5 4.5 collective-permute-start.1
  171.2 1.5 pad_maximum_fusion.3
  189.9 1.9 fusion.47
  202.4 1.6 maximum_select_fusion.12
  212.5 32.6 %all-reduce.4 = (f32[1,1]{1,0:T(1,128)}, f32[1,1]{1,0:T(1,128)}, f32[1,1]{1,0:T(1,128)}, f32[1,1]{1,0:T(1,128)}) all-reduce(f32[1,1]{1,0:T(1,128)} %bitcast.259, f32[1,1]{1,0:T(1,128)} %bitcast.256, f32[1,1]{1,0:T(1,128)} %bitcast.260, f32[1,1]{1,0:T(1,128)} %bitcast.154), channel_id=1, replica_groups=mesh['kpt'=2,'px'=16] {'px'}, use_global_device_ids=true, to_apply=%region_3.4 | all-reduce | flops 4 | bytes 32 | tf_op jit(solution)/shard_map/psum | solution.py:288
  254.8 1.6 convolution_subtract_fusion.7
  259.9 10.4 %copy.2320 = f32[1,3,1,4,4096]{3,0,2,1,4:T(1,128)} copy(f32[1,3,1,4,4096]{4,3,1,2,0:T(4,128)S(1)} %stack.650) | data formatting | bytes 393216 | tf_op jit(solution)/shard_map/stack | solution.py:163
  270.3 10.1 %copy.2321 = f32[1,3,1,4,4096]{3,0,2,1,4:T(1,128)} copy(f32[1,3,1,4,4096]{4,3,1,2,0:T(4,128)S(1)} %stack.651) | data formatting | bytes 393216 | tf_op jit(solution)/shard_map/stack | solution.py:163
  280.5 16.6 %fusion.761 = f32[4096,3,1,2,4]{4,3,2,1,0:T(2,128)} fusion(f32[1,3,1,4,4096]{3,0,2,1,4:T(1,128)} %copy.2321, f32[1,3,1,4,4096]{3,0,2,1,4:T(1,128)} %copy.2320), kind=kLoop, calls=%fused_computation.1222 | loop fusion | flops 98304 | bytes 786432
  297.1 17.0 %reshape.14432 = f32[16,1,6144]{2,1,0:T(1,128)S(1)} reshape(f32[4096,3,1,2,4]{4,3,2,1,0:T(2,128)} %fusion.761) | data formatting | bytes 786432
  314.1 15.2 %all_to_all.90 = f32[16,1,6144]{2,1,0:T(1,128)S(1)} all-to-all(f32[16,1,6144]{2,1,0:T(1,128)S(1)} %reshape.14432), channel_id=1, replica_groups=mesh['kpt'=2,'px'=16] {'px'}, dimensions={0} | all-to-all | bytes 786432 | tf_op jit(solution)/shard_map/all_to_all | solution.py:263
  329.2 1.5 reduce.69
  330.7 24.8 %reshape.14433 = f32[4096,3,1,2,4]{4,3,2,1,0:T(2,128)} reshape(f32[16,6144]{1,0:T(8,128)S(1)} %reduce.69) | data formatting | bytes 786432
  355.5 15.5 %copy.2322 = f32[2,3,1,4,16,256]{5,3,4,1,2,0:T(4,128)S(1)} copy(f32[2,3,1,4,16,256]{3,0,1,5,4,2:T(2,128)} %bitcast.1770) | data formatting | bytes 786432 | tf_op jit(solution)/shard_map/all_to_all | solution.py:263
  375.9 15.5 %all_to_all.91 = f32[2,3,1,64,256]{4,0,2,1,3:T(2,128)S(1)} all-to-all(f32[2,3,1,64,256]{4,0,2,1,3:T(2,128)S(1)} %copy.2339), channel_id=1, replica_groups=mesh['kpt'=2,'px'=16] {'px'}, dimensions={3} | all-to-all | bytes 786432 | tf_op jit(solution)/shard_map/all_to_all | solution.py:265
  401.8 33.2 %all-reduce.3 = (f32[1,1]{1,0:T(1,128)}, f32[1,1]{1,0:T(1,128)}) all-reduce(f32[1,1]{1,0:T(1,128)} %bitcast.335, f32[1,1]{1,0:T(1,128)} %bitcast.334), channel_id=1, replica_groups=mesh['kpt'=2,'px'=16] {'px'}, use_global_device_ids=true, to_apply=%region_6.7 | all-reduce | flops 2 | bytes 16 | tf_op jit(solution)/shard_map/psum | solution.py:295
  444.4 4.6 collective-permute-start.4
  465.8 1.7 copy.2379
  467.5 1.7 copy.2370
  495.1 32.3 %all-reduce.2 = (f32[1,1]{1,0:T(1,128)}, f32[1,1]{1,0:T(1,128)}, f32[1,1]{1,0:T(1,128)}, f32[1,1]{1,0:T(1,128)}) all-reduce(f32[1,1]{1,0:T(1,128)} %bitcast.436, f32[1,1]{1,0:T(1,128)} %bitcast.431, f32[1,1]{1,0:T(1,128)} %bitcast.439, f32[1,1]{1,0:T(1,128)} %bitcast.348), channel_id=1, replica_groups=mesh['kpt'=2,'px'=16] {'px'}, use_global_device_ids=true, to_apply=%region_9.10 | all-reduce | flops 4 | bytes 32 | tf_op jit(solution)/shard_map/psum | solution.py:288
  541.3 10.4 %copy.2435 = f32[1,3,1,4,4096]{3,0,2,1,4:T(1,128)} copy(f32[1,3,1,4,4096]{4,3,1,2,0:T(4,128)S(1)} %stack.714) | data formatting | bytes 393216 | tf_op jit(solution)/shard_map/stack | solution.py:163
  551.7 10.1 %copy.2436 = f32[1,3,1,4,4096]{3,0,2,1,4:T(1,128)} copy(f32[1,3,1,4,4096]{4,3,1,2,0:T(4,128)S(1)} %stack.715) | data formatting | bytes 393216 | tf_op jit(solution)/shard_map/stack | solution.py:163
  561.8 16.6 %fusion.760 = f32[4096,3,1,2,4]{4,3,2,1,0:T(2,128)} fusion(f32[1,3,1,4,4096]{3,0,2,1,4:T(1,128)} %copy.2436, f32[1,3,1,4,4096]{3,0,2,1,4:T(1,128)} %copy.2435), kind=kLoop, calls=%fused_computation.1221 | loop fusion | flops 98304 | bytes 786432
  578.5 17.0 %reshape.14434 = f32[16,1,6144]{2,1,0:T(1,128)S(1)} reshape(f32[4096,3,1,2,4]{4,3,2,1,0:T(2,128)} %fusion.760) | data formatting | bytes 786432
  595.4 14.9 %all_to_all.92 = f32[16,1,6144]{2,1,0:T(1,128)S(1)} all-to-all(f32[16,1,6144]{2,1,0:T(1,128)S(1)} %reshape.14434), channel_id=1, replica_groups=mesh['kpt'=2,'px'=16] {'px'}, dimensions={0} | all-to-all | bytes 786432 | tf_op jit(solution)/shard_map/all_to_all | solution.py:263
  610.4 1.5 reduce.70
  611.9 24.8 %reshape.14435 = f32[4096,3,1,2,4]{4,3,2,1,0:T(2,128)} reshape(f32[16,6144]{1,0:T(8,128)S(1)} %reduce.70) | data formatting | bytes 786432
  636.7 15.5 %copy.2437 = f32[2,3,1,4,16,256]{5,3,4,1,2,0:T(4,128)S(1)} copy(f32[2,3,1,4,16,256]{3,0,1,5,4,2:T(2,128)} %bitcast.1771) | data formatting | bytes 786432 | tf_op jit(solution)/shard_map/all_to_all | solution.py:263
  657.1 15.5 %all_to_all.93 = f32[2,3,1,64,256]{4,0,2,1,3:T(2,128)S(1)} all-to-all(f32[2,3,1,64,256]{4,0,2,1,3:T(2,128)S(1)} %copy.2442), channel_id=1, replica_groups=mesh['kpt'=2,'px'=16] {'px'}, dimensions={3} | all-to-all | bytes 786432 | tf_op jit(solution)/shard_map/all_to_all | solution.py:265
  682.4 33.4 %all-reduce.1 = (f32[1,1]{1,0:T(1,128)}, f32[1,1]{1,0:T(1,128)}) all-reduce(f32[1,1]{1,0:T(1,128)} %bitcast.501, f32[1,1]{1,0:T(1,128)} %bitcast.500), channel_id=1, replica_groups=mesh['kpt'=2,'px'=16] {'px'}, use_global_device_ids=true, to_apply=%region_12.13 | all-reduce | flops 2 | bytes 16 | tf_op jit(solution)/shard_map/psum | solution.py:295
  727.9 4.6 collective-permute-start.6
  743.7 1.6 maximum_select_fusion.8
  751.4 2.4 fusion.56
  766.8 1.9 fusion.85
  777.2 32.3 %all-reduce = (f32[1,1]{1,0:T(1,128)}, f32[1,1]{1,0:T(1,128)}, f32[1,1]{1,0:T(1,128)}, f32[1,1]{1,0:T(1,128)}) all-reduce(f32[1,1]{1,0:T(1,128)} %bitcast.589, f32[1,1]{1,0:T(1,128)} %bitcast.584, f32[1,1]{1,0:T(1,128)} %bitcast.592, f32[1,1]{1,0:T(1,128)} %bitcast.514), channel_id=1, replica_groups=mesh['kpt'=2,'px'=16] {'px'}, use_global_device_ids=true, to_apply=%region_15.16 | all-reduce | flops 4 | bytes 32 | tf_op jit(solution)/shard_map/psum | solution.py:288
  (717 shorter events, 200.9 us)
Async XLA Ops:
  1.5 148.7 %collective-permute-start.2 = (s32[1,4096]{1,0:T(1,128)S(1)}, s32[1,4096]{1,0:T(1,128)S(1)}, u32[]{:S(2)}, u32[]{:S(2)}) collective-permute-start(s32[1,4096]{1,0:T(1,128)S(1)} %slice.1041), channel_id=1, source_target_pairs={{0,1},{1,2},{2,3},{3,4},{4,5},{5,6},{6,7},{7,8},{8,9},{9,10},{10,1... | collective-permute-start | bytes 49160 | tf_op jit(solution)/shard_map/ppermute | solution.py:18
  4.1 393.6 %copy-start.96 = (f32[64]{0:T(128)}, f32[64]{0:T(128)S(1)}, u32[]{:S(2)}) copy-start(f32[64]{0:T(128)S(1)} %multiply_multiply_fusion) | copy-start | bytes 772
  8.6 386.4 %copy-start.98 = (f32[64]{0:T(128)}, f32[64]{0:T(128)S(1)}, u32[]{:S(2)}) copy-start(f32[64]{0:T(128)S(1)} %multiply_multiply_fusion.2) | copy-start | bytes 772
  54.4 24.9 %copy-start.136 = (f32[3]{0:T(128)S(1)}, f32[3]{0:T(128)}, u32[]{:S(2)}) copy-start(f32[3]{0:T(128)} %param.7) | copy-start | bytes 40
  54.4 26.0 %copy-start.137 = (f32[2]{0:T(128)S(1)}, f32[2]{0:T(128)}, u32[]{:S(2)}) copy-start(f32[2]{0:T(128)} %param.9) | copy-start | bytes 28
  72.0 19.4 %all-to-all-start = ((f32[16,1,6144]{2,1,0:T(1,128)}), f32[16,1,6144]{2,1,0:T(1,128)S(1)}, u32[]{:S(2)}, u32[]{:S(2)}) async-start(f32[16,1,6144]{2,1,0:T(1,128)} %reshape.14430), calls=%async_computation | async-start | bytes 786432 | tf_op jit(solution)/shard_map/all_to_all | solution.py:263
  82.3 53.7 %copy-start.126 = (f32[64]{0:T(128)}, f32[64]{0:T(128)S(1)}, u32[]{:S(2)}) copy-start(f32[64]{0:T(128)S(1)} %get-tuple-element.318) | copy-start | bytes 772
  82.3 53.7 %copy-start.129 = (f32[64]{0:T(128)}, f32[64]{0:T(128)S(1)}, u32[]{:S(2)}) copy-start(f32[64]{0:T(128)S(1)} %get-tuple-element.319) | copy-start | bytes 772
  83.0 53.0 %copy-start.132 = (f32[64]{0:T(128)}, f32[64]{0:T(128)S(1)}, u32[]{:S(2)}) copy-start(f32[64]{0:T(128)S(1)} %get-tuple-element.321) | copy-start | bytes 772
  83.0 292.1 %copy-start.100 = (f32[64]{0:T(128)}, f32[64]{0:T(128)S(1)}, u32[]{:S(2)}) copy-start(f32[64]{0:T(128)S(1)} %get-tuple-element.320) | copy-start | bytes 772
  84.3 288.9 %copy-start.109 = (f32[256]{0:T(256)}, f32[256]{0:T(256)S(1)}, u32[]{:S(2)}) copy-start(f32[256]{0:T(256)S(1)} %get-tuple-element.323) | copy-start | bytes 3076
  84.3 288.9 %copy-start.111 = (f32[256]{0:T(256)}, f32[256]{0:T(256)S(1)}, u32[]{:S(2)}) copy-start(f32[256]{0:T(256)S(1)} %get-tuple-element.322) | copy-start | bytes 3076
  85.0 288.2 %copy-start.113 = (f32[256]{0:T(256)}, f32[256]{0:T(256)S(1)}, u32[]{:S(2)}) copy-start(f32[256]{0:T(256)S(1)} %get-tuple-element.314) | copy-start | bytes 3076
  85.0 288.2 %copy-start.115 = (f32[256]{0:T(256)}, f32[256]{0:T(256)S(1)}, u32[]{:S(2)}) copy-start(f32[256]{0:T(256)S(1)} %get-tuple-element.315) | copy-start | bytes 3076
  85.7 287.6 %copy-start.117 = (f32[256]{0:T(256)}, f32[256]{0:T(256)S(1)}, u32[]{:S(2)}) copy-start(f32[256]{0:T(256)S(1)} %get-tuple-element.316) | copy-start | bytes 3076
  85.7 287.6 %copy-start.119 = (f32[256]{0:T(256)}, f32[256]{0:T(256)S(1)}, u32[]{:S(2)}) copy-start(f32[256]{0:T(256)S(1)} %get-tuple-element.317) | copy-start | bytes 3076
  137.7 5.6 copy-start.108
  139.3 16.1 %all-to-all-start.1 = ((f32[2,3,1,64,256]{4,0,2,1,3:T(2,128)}), f32[2,3,1,64,256]{4,0,2,1,3:T(2,128)S(1)}, u32[]{:S(2)}, u32[]{:S(2)}) async-start(f32[2,3,1,64,256]{4,0,2,1,3:T(2,128)} %copy.2232), calls=%async_computation.1 | async-start | bytes 786432 | tf_op jit(solution)/shard_map/all_to_all | solution.py:265
  145.4 59.1 %copy-start.20 = (f32[4,64,64]{2,1,0:T(8,128)}, f32[4,64,64]{2,1,0:T(8,128)S(1)}, u32[]{:S(2)}) copy-start(f32[4,64,64]{2,1,0:T(8,128)S(1)} %reshape.14242) | copy-start | bytes 196612
  146.0 43.9 %copy-start.123 = (pred[64]{0:T(512)(128)(4,1)}, pred[64]{0:T(512)(128)(4,1)S(1)}, u32[]{:S(2)}) copy-start(pred[64]{0:T(512)(128)(4,1)S(1)} %iota_compare_fusion) | copy-start | bytes 196
  152.4 321.9 %copy-start.14 = (f32[5,64,64]{2,0,1:T(8,128)}, f32[5,64,64]{2,0,1:T(8,128)S(1)}, u32[]{:S(2)}) copy-start(f32[5,64,64]{2,0,1:T(8,128)S(1)} %copy.2823) | copy-start | bytes 245764
  161.5 5.0 copy-start.22
  162.5 8.5 %collective-permute-start = (f32[2,3,1,1,64,64]{5,3,4,2,1,0:T(1,128)S(1)}, f32[2,3,1,1,64,64]{5,3,4,2,1,0:T(1,128)S(1)}, u32[]{:S(2)}, u32[]{:S(2)}) collective-permute-start(f32[2,3,1,1,64,64]{5,3,4,2,1,0:T(1,128)S(1)} %get-tuple-element.141), channel_id=1, source_target_pairs={{0,1},{1,2},{2,3},{3,4},{4,5},{5,6},{6,7},{7,8},{8,9},{9,10},{10,1... | collective-permute-start | bytes 294920 | tf_op jit(solution)/shard_map/ppermute | solution.py:28
  166.5 22.2 %collective-permute-start.1 = (f32[2,3,1,1,64,64]{5,3,4,2,1,0:T(1,128)}, f32[2,3,1,1,64,64]{5,3,4,2,1,0:T(1,128)}, u32[]{:S(2)}, u32[]{:S(2)}) collective-permute-start(f32[2,3,1,1,64,64]{5,3,4,2,1,0:T(1,128)} %get-tuple-element.142), channel_id=1, source_target_pairs={{1,0},{2,1},{3,2},{4,3},{5,4},{6,5},{7,6},{8,7},{9,8},{10,9},{11,1... | collective-permute-start | bytes 294920 | tf_op jit(solution)/shard_map/ppermute | solution.py:29
  187.0 2.9 copy-start.33
  188.7 283.9 %copy-start.54 = (f32[1,3,1,1,64,64]{5,4,3,2,1,0:T(8,128)}, f32[1,3,1,1,64,64]{5,4,3,2,1,0:T(8,128)S(1)}, u32[]{:S(2)}) copy-start(f32[1,3,1,1,64,64]{5,4,3,2,1,0:T(8,128)S(1)} %mul.3410) | copy-start | bytes 147460
  398.3 41.0 %copy-start.43 = (f32[3,4,4096]{2,1,0:T(4,128)S(1)}, f32[3,4,4096]{2,1,0:T(4,128)}, u32[]{:S(2)}) copy-start(f32[3,4,4096]{2,1,0:T(4,128)} %reshape.14240) | copy-start | bytes 589828
  441.9 7.1 copy-start.88
  441.9 7.1 copy-start.89
  444.4 8.0 collective-permute-start.3
  444.4 28.2 %collective-permute-start.4 = (f32[2,3,1,1,64,64]{5,3,4,2,1,0:T(1,128)}, f32[2,3,1,1,64,64]{5,3,4,2,1,0:T(1,128)}, u32[]{:S(2)}, u32[]{:S(2)}) collective-permute-start(f32[2,3,1,1,64,64]{5,3,4,2,1,0:T(1,128)} %get-tuple-element.136), channel_id=1, source_target_pairs={{1,0},{2,1},{3,2},{4,3},{5,4},{6,5},{7,6},{8,7},{9,8},{10,9},{11,1... | collective-permute-start | bytes 294920 | tf_op jit(solution)/shard_map/ppermute | solution.py:29
  449.0 3.4 copy-start.57
  453.1 2.8 copy-start.3
  462.8 2.8 copy-start.106
  487.7 47.1 %copy-start.24 = (f32[1,3,1,4,4096]{4,3,1,2,0:T(4,128)S(1)}, f32[1,3,1,4,4096]{4,3,1,2,0:T(4,128)}, u32[]{:S(2)}) copy-start(f32[1,3,1,4,4096]{4,3,1,2,0:T(4,128)} %copy-done.23) | copy-start | bytes 589828
  487.7 47.1 %copy-start.27 = (f32[1,3,1,4,4096]{4,3,1,2,0:T(4,128)S(1)}, f32[1,3,1,4,4096]{4,3,1,2,0:T(4,128)}, u32[]{:S(2)}) copy-start(f32[1,3,1,4,4096]{4,3,1,2,0:T(4,128)} %copy-done.26) | copy-start | bytes 589828
  636.7 15.7 %copy-start.101 = (f32[64]{0:T(128)S(1)}, f32[64]{0:T(128)}, u32[]{:S(2)}) copy-start(f32[64]{0:T(128)} %copy-done.100) | copy-start | bytes 772
  723.6 8.9 %collective-permute-start.5 = (f32[2,3,1,1,64,64]{5,3,4,2,1,0:T(1,128)S(1)}, f32[2,3,1,1,64,64]{5,3,4,2,1,0:T(1,128)S(1)}, u32[]{:S(2)}, u32[]{:S(2)}) collective-permute-start(f32[2,3,1,1,64,64]{5,3,4,2,1,0:T(1,128)S(1)} %copy.2808), channel_id=1, source_target_pairs={{0,1},{1,2},{2,3},{3,4},{4,5},{5,6},{6,7},{7,8},{8,9},{9,10},{10,1... | collective-permute-start | bytes 294920 | tf_op jit(solution)/shard_map/ppermute | solution.py:28
  723.7 8.8 %copy-start.58 = (f32[1,3,1,1,64,64]{5,4,3,2,1,0:T(8,128)S(1)}, f32[1,3,1,1,64,64]{5,4,3,2,1,0:T(8,128)}, u32[]{:S(2)}) copy-start(f32[1,3,1,1,64,64]{5,4,3,2,1,0:T(8,128)} %copy-done.56) | copy-start | bytes 147460
  727.9 22.4 %collective-permute-start.6 = (f32[2,3,1,1,64,64]{5,3,0,4,2,1:T(1,128)}, f32[2,3,1,1,64,64]{5,3,0,4,2,1:T(1,128)}, u32[]{:S(2)}, u32[]{:S(2)}) collective-permute-start(f32[2,3,1,1,64,64]{5,3,0,4,2,1:T(1,128)} %get-tuple-element.131), channel_id=1, source_target_pairs={{1,0},{2,1},{3,2},{4,3},{5,4},{6,5},{7,6},{8,7},{9,8},{10,9},{11,1... | collective-permute-start | bytes 294920 | tf_op jit(solution)/shard_map/ppermute | solution.py:29
  736.2 2.9 copy-start.9
  746.3 4.0 copy-start.55
  747.0 4.4 copy-start.10
  762.7 3.3 copy-start.62
  770.4 46.4 %copy-start.25 = (f32[1,3,1,4,4096]{4,3,1,2,0:T(4,128)S(1)}, f32[1,3,1,4,4096]{4,3,1,2,0:T(4,128)}, u32[]{:S(2)}) copy-start(f32[1,3,1,4,4096]{4,3,1,2,0:T(4,128)} %copy-done.23) | copy-start | bytes 589828
  770.4 46.4 %copy-start.28 = (f32[1,3,1,4,4096]{4,3,1,2,0:T(4,128)S(1)}, f32[1,3,1,4,4096]{4,3,1,2,0:T(4,128)}, u32[]{:S(2)}) copy-start(f32[1,3,1,4,4096]{4,3,1,2,0:T(4,128)} %copy-done.26) | copy-start | bytes 589828
  770.4 46.4 %copy-start.45 = (f32[1,3,1,4,4096]{4,3,1,2,0:T(4,128)S(1)}, f32[1,3,1,4,4096]{4,3,1,2,0:T(4,128)}, u32[]{:S(2)}) copy-start(f32[1,3,1,4,4096]{4,3,1,2,0:T(4,128)} %copy-done.44) | copy-start | bytes 589828
  770.4 46.4 %copy-start.47 = (f32[1,3,1,4,4096]{4,3,1,2,0:T(4,128)S(1)}, f32[1,3,1,4,4096]{4,3,1,2,0:T(4,128)}, u32[]{:S(2)}) copy-start(f32[1,3,1,4,4096]{4,3,1,2,0:T(4,128)} %copy-done.46) | copy-start | bytes 589828
  (99 other events, 160.8 us)
where the time goes:
time: 831 us; the launch traced here: 819 us
  local copies, waits for them, and re-layouts  320 us (39%)
  blocking collectives  225 us (27%)
  other arithmetic  140 us (17%)
  between operations  51.9 us (6%)
  matrix products  48.9 us (6%)
  starting transfers between devices  25.6 us (3%)
    unnamed x312, local copies, waits for them, and re-layouts  143 us
    psum x3, blocking collectives, on_device(): lax.psum((first_pair[0], first_pair[1], second_pair[0], second_pair[1]),...  97.3 us
    another operation x20, local copies, waits for them, and re-layouts, contract(): return jnp.stack([real_part, imag_part])  67.3 us
    psum x2, blocking collectives, on_device(): update_totals = lax.psum((update_pair[0], update_pair[1]), 'px')  66.5 us
    unnamed x5, other arithmetic  51.8 us
    all_to_all x4, local copies, waits for them, and re-layouts, precondition(): lax.all_to_all(flat_spectrum, 'px', split_axis=4, concat_axis=3, tiled=True)  46.9 us
    all_to_all x2, blocking collectives, precondition(): lax.all_to_all(worked, 'px', split_axis=3, concat_axis=4, tiled=True)  31 us
    all_to_all x2, blocking collectives, precondition(): lax.all_to_all(flat_spectrum, 'px', split_axis=4, concat_axis=3, tiled=True)  30.1 us
  transfers between devices with their start and end apart: 9, of which 2 were waited for; matrix products, arithmetic and copies ran while one was open for 23% of the time, Pallas kernels for 0%

commit v1 on v0

v1 whole, which is shorter than its diff:
```python
import functools
import math

import jax
import jax.numpy as jnp
from jax import lax
from jax.experimental import pallas as pl
from jax.experimental.pallas import tpu as pltpu
from jax.sharding import PartitionSpec as P

ITERS = 3
PRECISE = lax.Precision.HIGHEST
MESH = pl.DeviceIdType.MESH


def material_scale(material, permittivity):
    scaled = jnp.zeros(material.shape, jnp.float32)
    for material_id in range(permittivity.shape[0]):
        scaled = scaled + jnp.where(
            material == material_id, permittivity[material_id], jnp.float32(0.0)
        )
    return scaled


def transform_table(theta, size, forward):
    modes = lax.broadcasted_iota(jnp.int32, (size, size), 0)
    cells = lax.broadcasted_iota(jnp.int32, (size, size), 1)
    angles = (
        2.0 * math.pi * (modes * cells % size).astype(jnp.float32) / size
        + theta * cells.astype(jnp.float32) / size
    )
    if forward:
        return jnp.cos(angles), -jnp.sin(angles)
    return jnp.cos(angles).T / size, jnp.sin(angles).T / size


def right_table(table):
    real, imag = table[0].T, table[1].T
    plain = jnp.concatenate(
        [jnp.concatenate([real, imag], 1), jnp.concatenate([-imag, real], 1)], 0
    )
    turned = jnp.concatenate(
        [jnp.concatenate([-imag, real], 1), jnp.concatenate([-real, -imag], 1)], 0
    )
    return jnp.concatenate([plain, turned], 1)


def left_table(table):
    return jnp.concatenate([table[0], table[1]], 1)


def dot(a, b):
    return lax.dot_general(
        a, b, (((1,), (0,)), ((), ())), precision=PRECISE, preferred_element_type=jnp.float32
    )


def kernel_body(
    count,
    planes,
    size,
    pad,
    scal,
    right,
    permit,
    rzf,
    lyf,
    lxf,
    rzi,
    lyi,
    lxi,
    lanes,
    dx,
    gain,
    sol_out,
    res_out,
    send,
    recv,
    precond,
    direc,
    image,
    curl_buf,
    operated,
    low_permit,
    inv_low,
    inv_eps,
    low_halo,
    up_halo,
    part_send,
    part_recv,
    a2a_send_sem,
    a2a_recv_sem,
    part_send_sem,
    part_recv_sem,
    halo_send_sem,
    halo_recv_sem,
):
    me = lax.axis_index("px")
    kys = size // count
    chunk = pad * planes * kys
    half = size

    def peer(k):
        return lax.rem(me + k, count)

    barrier = pltpu.get_barrier_semaphore()

    def greet(k, carry):
        pl.semaphore_signal(
            barrier, inc=1, device_id={"px": peer(k)}, device_id_type=MESH
        )
        return carry

    lax.fori_loop(1, count, greet, 0)
    pl.semaphore_wait(barrier, count - 1)

    sign = lanes[2:3, :]
    zfa, zfb, zba, zbb = (lanes[i : i + 1, :] for i in range(3, 7))
    dz_re, dz_im = lanes[0:1, :], lanes[1:2, :]

    def turn(f):
        return pltpu.roll(f, half, f.ndim - 1) * sign

    def cmul(re, im, f):
        return re * f + im * turn(f)

    def copy_to(src, dst, ssem, rsem, target):
        return pltpu.make_async_remote_copy(
            src_ref=src,
            dst_ref=dst,
            send_sem=ssem,
            recv_sem=rsem,
            device_id={"px": target},
            device_id_type=MESH,
        )

    def rows(dev):
        return pl.ds(pl.multiple_of(dev * chunk, 8), chunk)

    def exchange_copy(e, par, k):
        return copy_to(
            send.at[e, rows(peer(k))],
            recv.at[e, rows(me)],
            a2a_send_sem.at[par, k],
            a2a_recv_sem.at[par, k],
            peer(k),
        )

    def exchange(e, par):
        def start(k, carry):
            exchange_copy(e, par, k).start()
            return carry

        def finish(k, carry):
            exchange_copy(e, par, k).wait()
            return carry

        lax.fori_loop(1, count, start, 0)
        recv[e, rows(me), :] = send[e, rows(me), :]
        lax.fori_loop(1, count, finish, 0)

    def part_copy(e, k):
        return copy_to(
            part_send.at[e],
            part_recv.at[e, me],
            part_send_sem.at[lax.rem(e, 2), k],
            part_recv_sem.at[lax.rem(e, 2), k],
            peer(k),
        )

    def part_start(e):
        def start(k, carry):
            part_copy(e, k).start()
            return carry

        lax.fori_loop(1, count, start, 0)
        part_recv[e, me] = part_send[e]

    def part_finish(e):
        def finish(k, carry):
            part_copy(e, k).wait()
            return carry

        lax.fori_loop(1, count, finish, 0)
        total = part_recv[e, 0]
        for s in range(1, count):
            total = total + part_recv[e, s]
        return jnp.sum(total, axis=1, keepdims=True)

    permit_copy = copy_to(
        permit.at[planes - 1],
        low_permit,
        halo_send_sem.at[0],
        halo_recv_sem.at[0],
        peer(1),
    )
    permit_copy.start()
    inv_eps[...] = 1.0 / permit[...]

    def halo_copies(it):
        low = copy_to(
            precond.at[it, :, planes - 1],
            low_halo.at[it],
            halo_send_sem.at[1],
            halo_recv_sem.at[1],
            peer(1),
        )
        up = copy_to(
            precond.at[it, 1:3, 0],
            up_halo.at[it],
            halo_send_sem.at[2],
            halo_recv_sem.at[2],
            lax.rem(me + count - 1, count),
        )
        return low, up

    def spectrum_forward(e):
        for c in range(3):
            for x in range(planes):
                both = dot(image[c, x], rzf[...])
                mixed = jnp.concatenate([both[:, : 2 * half], both[:, 2 * half :]], 0)
                out = dot(lyf[...], mixed)
                for d in range(count):
                    at = d * chunk + (x * pad + c) * kys
                    send[e, at : at + kys, :] = out[d * kys : (d + 1) * kys, :]

    def columns_work(e):
        for k in range(kys):
            dy_re, dy_im = scal[8 + 2 * k], scal[9 + 2 * k]
            dx_re, dx_im = dx[0], dx[1]
            spec = []
            inner = None
            factors = [(dx_re, dx_im), (dy_re, dy_im), (dz_re, dz_im)]
            for c in range(3):
                g = recv[e, pl.ds(c * kys + k, size, stride=pad * kys), :]
                w = dot(lxf[...], jnp.concatenate([g, turn(g)], 0))
                spec.append(w)
                term = factors[c][0] * w - factors[c][1] * turn(w)
                inner = term if inner is None else inner + term
            scale = gain[k]
            inner = inner * (scale * scal[6])
            inner_turned = turn(inner)
            for c in range(3):
                u = spec[c] * scale + factors[c][0] * inner + factors[c][1] * inner_turned
                out = dot(lxi[...], jnp.concatenate([u, turn(u)], 0))
                for d in range(count):
                    at = d * chunk + (k * pad + c) * planes
                    send[e + 1, at : at + planes, :] = out[d * planes : (d + 1) * planes, :]

    def field_back(e, c, x):
        v = recv[e + 1, pl.ds(c * planes + x, size, stride=pad * planes), :]
        both = dot(v, rzi[...])
        mixed = jnp.concatenate([both[:, : 2 * half], both[:, 2 * half :]], 0)
        return dot(lyi[...], mixed)

    cos_y, sin_y = scal[0], scal[1]
    cos_up, sin_up, cos_dn, sin_dn = scal[2], scal[3], scal[4], scal[5]
    q0, q1 = scal[7], scal[8 + 2 * kys]
    row = lax.broadcasted_iota(jnp.int32, (size, 2 * half), 0)

    def next_y(f):
        edge = cmul(cos_y, sin_y, f[0:1])
        return jnp.where(row == size - 1, edge, pltpu.roll(f, size - 1, 0))

    def prev_y(f):
        edge = cmul(cos_y, -sin_y, f[size - 1 : size])
        return jnp.where(row == 0, edge, pltpu.roll(f, 1, 0))

    def next_z(f):
        return pltpu.roll(f, 2 * half - 1, 1) * zfa + pltpu.roll(f, half - 1, 1) * zfb

    def prev_z(f):
        return pltpu.roll(f, 1, 1) * zba + pltpu.roll(f, half + 1, 1) * zbb

    def operate(it):
        for x in range(-1, planes):
            if x < 0:
                e = [cmul(cos_dn, sin_dn, low_halo[it, c]) for c in range(3)]
                inv = inv_low[...]
            else:
                e = [precond[it, c, x] for c in range(3)]
                inv = inv_eps[x]
            if x + 1 < planes:
                up_y, up_z = precond[it, 1, x + 1], precond[it, 2, x + 1]
            else:
                up_y, up_z = (cmul(cos_up, sin_up, up_halo[it, c]) for c in range(2))
            curl_buf[1, x + 1] = ((next_z(e[0]) - e[0]) - (up_z - e[2])) * inv
            curl_buf[2, x + 1] = ((up_y - e[1]) - (next_y(e[0]) - e[0])) * inv
            if x >= 0:
                curl_buf[0, x + 1] = (
                    (next_y(e[2]) - e[2]) - (next_z(e[1]) - e[1])
                ) * inv
        for x in range(planes):
            h = [curl_buf[c, x + 1] for c in range(3)]
            low_y, low_z = curl_buf[1, x], curl_buf[2, x]
            parts = [
                (prev_z(h[1]) - h[1]) - (prev_y(h[2]) - h[2]),
                (low_z - h[2]) - (prev_z(h[0]) - h[0]),
                (prev_y(h[0]) - h[0]) - (low_y - h[1]),
            ]
            for c in range(3):
                operated[c, x] = parts[c] + cmul(q0, q1, precond[it, c, x]) * permit[x]

    def solve(g_re, g_im, s_re, s_im):
        factor = g_im / g_re
        low = (s_im - factor * s_re) / (g_re + factor * g_im)
        return (s_re + g_im * low) / g_re, low

    def folded(value):
        return jnp.sum(value, axis=0, keepdims=True)

    image[...] = right[...]
    res_out[...] = right[...]
    sol_out[...] = jnp.zeros_like(sol_out)
    direc[...] = jnp.zeros_like(direc)

    def update(coef_re, coef_im):
        for c in range(3):
            for x in range(planes):
                sol_out[c, x] = sol_out[c, x] + cmul(coef_re, coef_im, direc[c, x])
                res_out[c, x] = res_out[c, x] - cmul(coef_re, coef_im, image[c, x])

    def gram_totals(it):
        totals = part_finish(2 * it - 1)
        return totals[0:1], totals[1:2], totals[2:3], totals[3:4]

    def iteration(it, carry):
        e = 2 * it
        spectrum_forward(e)
        exchange(e, 0)
        columns_work(e)
        exchange(e + 1, 1)

        @pl.when(it == 0)
        def _():
            for c in range(3):
                for x in range(planes):
                    precond[it, c, x] = field_back(e, c, x)
            for copy in halo_copies(it):
                copy.start()
            permit_copy.wait()
            inv_low[...] = 1.0 / low_permit[...]
            for copy in halo_copies(it):
                copy.wait()
            operate(it)
            for c in range(3):
                for x in range(planes):
                    direc[c, x] = precond[it, c, x]
                    image[c, x] = operated[c, x]

        @pl.when(it > 0)
        def _():
            g_re, g_im, s_re, s_im = gram_totals(it)
            coef_re, coef_im = solve(g_re, g_im, s_re, s_im)
            sum_re = jnp.zeros((size, 2 * half), jnp.float32)
            sum_im = jnp.zeros((size, 2 * half), jnp.float32)
            for c in range(3):
                for x in range(planes):
                    back = field_back(e, c, x)
                    value = precond[it - 1, c, x] - cmul(coef_re, coef_im, back)
                    precond[it, c, x] = value
                    sum_re = sum_re + image[c, x] * value
                    sum_im = sum_im - image[c, x] * turn(value)
            for copy in halo_copies(it):
                copy.start()
            part_send[2 * it, 0:1] = folded(sum_re)
            part_send[2 * it, 1:2] = folded(sum_im)
            part_start(2 * it)
            update(coef_re, coef_im)
            for copy in halo_copies(it):
                copy.wait()
            operate(it)
            totals = part_finish(2 * it)
            beta_re, beta_im = solve(g_re, g_im, totals[0:1], totals[1:2])
            for c in range(3):
                for x in range(planes):
                    direc[c, x] = precond[it, c, x] - cmul(beta_re, beta_im, direc[c, x])
                    image[c, x] = operated[c, x] - cmul(beta_re, beta_im, image[c, x])

        sums = [jnp.zeros((size, 2 * half), jnp.float32) for _ in range(4)]
        for c in range(3):
            for x in range(planes):
                d, m, r = direc[c, x], image[c, x], res_out[c, x]
                td = turn(d)
                sums[0] = sums[0] + d * m
                sums[1] = sums[1] + td * m
                sums[2] = sums[2] + d * r
                sums[3] = sums[3] + td * r
        for i in range(4):
            part_send[2 * it + 1, i : i + 1] = folded(sums[i])
        part_start(2 * it + 1)
        return carry

    part_send[...] = jnp.zeros_like(part_send)
    lax.fori_loop(0, ITERS, iteration, 0)
    update(*solve(*gram_totals(ITERS)))


def on_device(right_side, material, permittivity, bloch_phase, quad_shift):
    planes = right_side.shape[3]
    count = lax.axis_size("px")
    size = planes * count
    kys = size // count
    pad = 3
    while (pad * planes * kys) % 8:
        pad += 1
    position = lax.axis_index("px")
    f32 = jnp.float32

    permit = material_scale(material, permittivity).reshape(planes, size, size)
    permit = jnp.concatenate([permit, permit], 2)
    damping = quad_shift[0] * jnp.mean(permittivity)
    cosines, sines = jnp.cos(bloch_phase), jnp.sin(bloch_phase)
    is_top = position == count - 1
    is_bottom = position == 0
    modes = jnp.arange(size).astype(f32)
    kappas = [(2.0 * math.pi * modes + bloch_phase[a]) / size for a in range(3)]
    diffs = [(jnp.cos(kappa) - 1.0, jnp.sin(kappa)) for kappa in kappas]
    mine = [lax.dynamic_slice(part, (position * kys,), (kys,)) for part in diffs[1]]
    scal = jnp.concatenate(
        [
            jnp.stack(
                [
                    cosines[1],
                    sines[1],
                    jnp.where(is_top, cosines[0], 1.0),
                    jnp.where(is_top, sines[0], 0.0),
                    jnp.where(is_bottom, cosines[0], 1.0),
                    jnp.where(is_bottom, -sines[0], 0.0),
                    1.0 / damping,
                    quad_shift[0],
                ]
            ),
            jnp.stack(mine, 1).reshape(2 * kys),
            quad_shift[1:2],
        ]
    )
    squares = [re**2 + im**2 for re, im in diffs]
    mine_square = lax.dynamic_slice(squares[1], (position * kys,), (kys,))
    twice = lambda v: jnp.concatenate([v, v])
    gain = 1.0 / (
        squares[0][None, :, None]
        + mine_square[:, None, None]
        + twice(squares[2])[None, None, :]
        + damping
    )
    lane = jnp.arange(2 * size)
    low = lane < size
    last = lane % size == size - 1
    first = lane % size == 0
    lanes = jnp.stack(
        [
            twice(diffs[2][0]),
            twice(diffs[2][1]),
            jnp.where(low, -1.0, 1.0),
            jnp.where(last, jnp.where(low, -sines[2], sines[2]), 1.0),
            jnp.where(last, cosines[2], 0.0),
            jnp.where(first, jnp.where(low, sines[2], -sines[2]), 1.0),
            jnp.where(first, cosines[2], 0.0),
            jnp.zeros((2 * size,), f32),
        ]
    )
    dx = jnp.broadcast_to(jnp.stack(diffs[0])[:, :, None], (2, size, 2 * size))
    forward = [transform_table(bloch_phase[a], size, True) for a in range(3)]
    inverse = [transform_table(bloch_phase[a], size, False) for a in range(3)]
    field = right_side.reshape(2, 3, planes, size, size).transpose(1, 2, 3, 0, 4)
    field = field.reshape(3, planes, size, 2 * size)

    vmem = pl.BlockSpec(memory_space=pltpu.VMEM)
    fields = lambda n: pltpu.VMEM((3, n, size, 2 * size), f32)
    plane = (size, 2 * size)
    all_rows = count * pad * planes * kys
    dma = pltpu.SemaphoreType.DMA
    out = jax.ShapeDtypeStruct((3, planes, size, 2 * size), f32)
    solved, left = pl.pallas_call(
        functools.partial(kernel_body, count, planes, size, pad),
        out_shape=(out, out),
        in_specs=[pl.BlockSpec(memory_space=pltpu.SMEM)] + [vmem] * 11,
        out_specs=(vmem, vmem),
        scratch_shapes=[
            pltpu.VMEM((2 * ITERS, all_rows, 2 * size), f32),
            pltpu.VMEM((2 * ITERS, all_rows, 2 * size), f32),
            pltpu.VMEM((ITERS, 3, planes) + plane, f32),
            fields(planes),
            fields(planes),
            fields(planes + 1),
            fields(planes),
            pltpu.VMEM(plane, f32),
            pltpu.VMEM(plane, f32),
            pltpu.VMEM((planes,) + plane, f32),
            pltpu.VMEM((ITERS, 3) + plane, f32),
            pltpu.VMEM((ITERS, 2) + plane, f32),
            pltpu.VMEM((2 * ITERS, 8, 2 * size), f32),
            pltpu.VMEM((2 * ITERS, count, 8, 2 * size), f32),
            dma((2, count)),
            dma((2, count)),
            dma((2, count)),
            dma((2, count)),
            dma((3,)),
            dma((3,)),
        ],
        compiler_params=pltpu.CompilerParams(
            collective_id=0, has_side_effects=True, vmem_limit_bytes=60 * 2**20
        ),
    )(
        scal,
        field,
        permit,
        right_table(forward[2]),
        left_table(forward[1]),
        left_table(forward[0]),
        right_table(inverse[2]),
        left_table(inverse[1]),
        left_table(inverse[0]),
        lanes,
        dx,
        gain,
    )

    def restored(value):
        value = value.reshape(3, planes, size, 2, size).transpose(3, 0, 1, 2, 4)
        return value.reshape(right_side.shape)

    return restored(solved), restored(left)


def solution(mesh):
    return jax.shard_map(
        on_device,
        mesh=mesh,
        in_specs=(P(None, None, "kpt", "px", None), P("px", None), P(), P("kpt"), P()),
        out_specs=(P(None, None, "kpt", "px", None), P(None, None, "kpt", "px", None)),
        check_vma=False,
    )
```

time: 831 us -> 148 us (0.18); the launches traced: 819 us -> 147 us
  local copies, waits for them, and re-layouts: 320 us -> 17.6 us
  blocking collectives: 225 us -> 0 us
  other arithmetic: 140 us -> 16 us
  Pallas kernels: 0 us -> 108 us
  matrix products: 48.9 us -> 0 us
  between operations: 51.9 us -> 5.32 us
  starting transfers between devices: 25.6 us -> 0 us
    psum x5 -> x0, blocking collectives: 164 us -> none  [the longest x3 97.3 us: on_device(): lax.psum((first_pair[0], first_pair[1], second_pair[0], second_pair[1]),...]
    unnamed x312 -> x10, local copies, waits for them, and re-layouts: 143 us -> 1.97 us
    pallas_call x0 -> x1, Pallas kernels: none -> 108 us  [on_device(): pl.pallas_call(functools.partial(kernel_body, count, planes, size, pad),...]
    another operation x62 -> x4, local copies, waits for them, and re-layouts: 80.1 us -> 0.86 us  [the longest x1 0.61 us: on_device(): jnp.stack([twice(diffs[2][0]), twice(diffs[2][1]), jnp.where(low, -1.0, 1...]
    all_to_all x4 -> x0, blocking collectives: 61.1 us -> none  [the longest x2 31 us: precondition(): lax.all_to_all(worked, 'px', split_axis=3, concat_axis=4, tiled=True)]
    unnamed x5 -> x0, other arithmetic: 51.8 us -> none
    dot_general x72 -> x0, matrix products: 48.9 us -> none  [the longest x18 12.8 us: contract(): jnp.einsum(pattern, fields[1], tables[1], precision=PRECISE)]
    all_to_all x7 -> x0, local copies, waits for them, and re-layouts: 47.2 us -> none  [the longest x4 46.9 us: precondition(): lax.all_to_all(flat_spectrum, 'px', split_axis=4, concat_axis=3, tiled=True)]
  transfers between devices with their start and end apart: 9 -> 0, of which waited for: 2 -> 0; matrix products, arithmetic and copies ran while one was open for 23% -> 0% of each run, Pallas kernels for 0% -> 0%
where the time goes in v1:
time: 148 us; the launch traced here: 147 us
  Pallas kernels  108 us (73%)
  local copies, waits for them, and re-layouts  17.6 us (12%)
  other arithmetic  16 us (11%)
  between operations  5.32 us (4%)
    pallas_call x1, Pallas kernels, on_device(): pl.pallas_call(functools.partial(kernel_body, count, planes, size, pad),...  108 us
    concatenate x1, local copies, waits for them, and re-layouts, on_device(): jnp.concatenate([jnp.stack([cosines[1], sines[1], jnp.where(is_top, cosin...  3.2 us

profile of v1, /device:TPU:0, one launch (start us, length us, event | category | flops | bytes accessed | tf_op | source)
XLA Modules:
  0.0 147.4 jit_solution(3297459811740633769)
XLA Ops:
  0.6 0.7 fusion.19
  1.3 0.7 fusion.14
  4.6 0.6 copy-done.4
  5.2 0.6 fusion.18
  5.8 0.7 copy-done.3
  6.5 0.6 reduce_sum.9
  8.5 0.6 copy-done.2
  9.1 0.6 fusion.16
  9.7 0.6 cosine_add_fusion.2
  10.4 0.1 dynamic-slice_bitcast_fusion
  10.6 0.1 copy.11
  10.7 0.1 reshape.161
  10.7 3.2 %concatenate.65.scal = f32[17]{0:T(128)} concatenate(f32[1]{0:T(128)} %get-tuple-element.8, f32[1]{0:T(128)} %get-tuple-element.38, f32[1]{0:T(128)} %bitcast.1, f32[1]{0:T(128)} %bitcast.3, f32[1]{0:T(128)} %bitcast.4, f32[1]{0:T(128)} %bitcast.5, f32[1]{0:T(128)} %bitcast.7, f32[1]{0:T(128)} %get-tuple-element.35, f32[8]{0:T(128)S(1)} %reshape.161, f32[1]{0:T(128)} %get-tuple-element.34), dimensions={0} | concatenate | bytes 136 | tf_op jit(solution)/shard_map/concatenate | solution.py:420
  13.9 1.4 reshape.162
  15.3 0.6 copy.16
  16.0 1.2 reshape.163.right
  17.2 0.6 fusion.17
  17.8 1.9 %select_add_fusion = f32[4,4096]{1,0:T(4,128)S(1)} fusion(s32[4,4096]{1,0:T(4,128)S(1)} %copy-done.1, f32[]{:T(128)} %bitcast.14, f32[]{:T(128)} %bitcast.13, f32[]{:T(128)} %bitcast.12), kind=kLoop, calls=%fused_computation.5 | loop fusion | flops 131072 | bytes 131084 | tf_op jit(solution)/shard_map/add | solution.py:19
  19.7 0.1 reshape.164
  19.8 0.8 pad_maximum_fusion.permit
  20.6 0.7 multiply_multiply_fusion.2
  21.2 0.3 sine_multiply_fusion.2
  21.5 0.8 maximum_maximum_fusion.rzf
  22.3 0.6 multiply_add_fusion.1
  22.9 0.3 cosine_multiply_fusion.1
  23.2 0.7 pad_maximum_fusion.1.lyf
  23.9 0.7 multiply_add_fusion.2
  24.6 0.3 cosine_multiply_fusion
  24.8 0.7 pad_maximum_fusion.2.lxf
  25.5 0.8 maximum_maximum_fusion.1.rzi
  26.3 0.7 pad_maximum_fusion.3.lyi
  27.0 0.7 pad_maximum_fusion.4.lxi
  27.7 0.7 multiply_add_fusion
  29.1 0.6 compare_select_fusion.3
  29.7 0.7 compare_select_fusion.2
  30.3 0.6 compare_select_fusion.1
  30.9 0.7 compare_select_fusion
  31.6 0.6 stack.53.lanes
  32.2 0.7 cosine_add_fusion
  32.9 0.7 broadcast_in_dim.66.dx
  33.9 0.8 add_divide_fusion.gain
  34.6 108.5 %shard_map.68 = (f32[3,4,64,128]{3,2,1,0:T(8,128)}, f32[3,4,64,128]{3,2,1,0:T(8,128)}) custom-call(f32[17]{0:T(128)} %concatenate.65.scal, f32[3,4,64,128]{3,2,1,0:T(8,128)} %reshape.163.right, f32[4,64,128]{2,1,0:T(8,128)} %pad_maximum_fusion.permit, f32[128,256]{1,0:T(8,128)} %maximum_maximum_fusion.rzf, f32[64,128]{1,0:T(8,128)} %pad_maximum_fusion.1.lyf, ...), custom_call_target="tpu_custom_call" | custom-call | tf_op jit(solution)/shard_map/pallas_call | solution.py:475
  143.1 1.5 reshape.165
  144.6 0.1 copy.13
  144.7 1.1 reshape.166
  145.8 0.5 reshape.167
  146.2 0.1 copy.14
  146.3 1.1 reshape.168
  (17 shorter events, 0.5 us)
Async XLA Ops:
  4.6 0.7 copy-start.4
  5.8 0.7 copy-start.3
  8.5 0.7 copy-start.2
  16.0 1.8 %copy-start.1 = (s32[4,4096]{1,0:T(4,128)S(1)}, s32[4,4096]{1,0:T(4,128)}, u32[]{:S(2)}) copy-start(s32[4,4096]{1,0:T(4,128)} %param.6) | copy-start | bytes 196612
  144.7 1.1 copy-start

commit v2 on v1

v2 whole, which is shorter than its diff:
```python
import functools
import math

import jax
import jax.numpy as jnp
from jax import lax
from jax.experimental import pallas as pl
from jax.experimental.pallas import tpu as pltpu
from jax.sharding import PartitionSpec as P

ITERS = 3
PRECISE = lax.Precision.HIGHEST
MESH = pl.DeviceIdType.MESH


def dot(a, b):
    return lax.dot_general(
        a, b, (((1,), (0,)), ((), ())), precision=PRECISE, preferred_element_type=jnp.float32
    )


def kernel_body(
    count,
    planes,
    size,
    pad,
    kinds,
    permittivity,
    bloch,
    shift,
    right,
    material,
    sol_flat,
    res_flat,
    sol_out,
    res_out,
    permit,
    rzf,
    lyf,
    lxf,
    rzi,
    lyi,
    lxi,
    lanes,
    dx,
    gain,
    spec,
    inner_buf,
    send,
    recv,
    precond,
    direc,
    image,
    curl_buf,
    operated,
    low_permit,
    inv_low,
    inv_eps,
    low_halo,
    up_halo,
    part_send,
    part_recv,
    a2a_send_sem,
    a2a_recv_sem,
    part_send_sem,
    part_recv_sem,
    halo_send_sem,
    halo_recv_sem,
):
    me = lax.axis_index("px")
    kys = size // count
    chunk = planes * pad
    half = size

    def peer(k):
        return lax.rem(me + k, count)

    barrier = pltpu.get_barrier_semaphore()

    def greet(k, carry):
        pl.semaphore_signal(
            barrier, inc=1, device_id={"px": peer(k)}, device_id_type=MESH
        )
        return carry

    lax.fori_loop(1, count, greet, 0)

    def turn(f):
        return pltpu.roll(f, half, f.ndim - 1) * sign

    def cmul(re, im, f):
        return re * f + im * turn(f)

    def copy_to(src, dst, ssem, rsem, target):
        return pltpu.make_async_remote_copy(
            src_ref=src,
            dst_ref=dst,
            send_sem=ssem,
            recv_sem=rsem,
            device_id={"px": target},
            device_id_type=MESH,
        )

    def rows(dev):
        return pl.ds(pl.multiple_of(dev * chunk, 8), chunk)

    def exchange_copy(e, par, c, k):
        return copy_to(
            send.at[e, c, rows(peer(k))],
            recv.at[e, c, rows(me)],
            a2a_send_sem.at[par, c, k],
            a2a_recv_sem.at[par, c, k],
            peer(k),
        )

    def exchange_start(e, par, c):
        def start(k, carry):
            exchange_copy(e, par, c, k).start()
            return carry

        lax.fori_loop(1, count, start, 0)
        recv[e, c, rows(me), :] = send[e, c, rows(me), :]

    def exchange_finish(e, par, c):
        def finish(k, carry):
            exchange_copy(e, par, c, k).wait()
            return carry

        lax.fori_loop(1, count, finish, 0)

    def part_copy(e, k):
        return copy_to(
            part_send.at[e],
            part_recv.at[e, me],
            part_send_sem.at[lax.rem(e, 2), k],
            part_recv_sem.at[lax.rem(e, 2), k],
            peer(k),
        )

    def part_start(e):
        def start(k, carry):
            part_copy(e, k).start()
            return carry

        lax.fori_loop(1, count, start, 0)
        part_recv[e, me] = part_send[e]

    def part_finish(e):
        def finish(k, carry):
            part_copy(e, k).wait()
            return carry

        lax.fori_loop(1, count, finish, 0)
        total = part_recv[e, 0]
        for s in range(1, count):
            total = total + part_recv[e, s]
        return jnp.sum(total, axis=1, keepdims=True)


    wide = (size, 2 * half)
    row = lax.broadcasted_iota(jnp.int32, wide, 0)
    lane = lax.broadcasted_iota(jnp.int32, wide, 1)
    low = lane < half
    index = jnp.where(low, lane, lane - half)
    quarter = jnp.where(low, 0.0, 0.5 * math.pi)
    minus_high = jnp.where(low, 1.0, -1.0)
    minus_low = -minus_high
    base = (2.0 * math.pi / size) * lax.rem(row * index, size).astype(jnp.float32) - quarter
    sign = minus_low[0:1]

    def swap(f):
        return pltpu.roll(f, half, 1)

    def by_mode(axis):
        return jnp.cos(base + bloch[axis] * index.astype(jnp.float32) / size)

    def by_cell(axis):
        return jnp.cos(base + bloch[axis] * row.astype(jnp.float32) / size)

    lxf[...] = by_mode(0) * minus_high
    lyf[...] = by_mode(1) * minus_high
    lxi[...] = by_cell(0) / size
    lyi[...] = by_cell(1) / size
    cells = by_cell(2)
    rzf[0:half, 0 : 2 * half] = cells * minus_high
    rzf[0:half, 2 * half :] = swap(cells)
    rzf[half:, 0 : 2 * half] = swap(cells)
    rzf[half:, 2 * half :] = cells * minus_low
    modes = by_mode(2) / size
    rzi[0:half, 0 : 2 * half] = modes
    rzi[0:half, 2 * half :] = swap(modes) * minus_low
    rzi[half:, 0 : 2 * half] = swap(modes) * minus_low
    rzi[half:, 2 * half :] = -modes

    kappa_x = (2.0 * math.pi * row.astype(jnp.float32) + bloch[0]) / size
    dx[0] = jnp.cos(kappa_x) - 1.0
    dx[1] = jnp.sin(kappa_x)
    short = (lanes.shape[1], 2 * half)
    line = lax.broadcasted_iota(jnp.int32, short, 0)
    place = lax.broadcasted_iota(jnp.int32, short, 1)
    place = jnp.where(place < half, place, place - half)
    angles = (2.0 * math.pi * place.astype(jnp.float32) + bloch[2]) / size
    for axis in range(3):
        angles = jnp.where(line == axis, bloch[axis], angles)
    for k in range(kys):
        ky = (me * kys + k).astype(jnp.float32)
        angles = jnp.where(line == 4 + k, (2.0 * math.pi * ky + bloch[1]) / size, angles)
    lanes[0] = jnp.cos(angles)
    lanes[1] = jnp.sin(angles)

    def wave(i):
        return lanes[0, i : i + 1, :], lanes[1, i : i + 1, :]

    def difference(i):
        return lanes[0, i : i + 1, :] - 1.0, lanes[1, i : i + 1, :]

    mean = permittivity[0]
    for i in range(1, kinds):
        mean = mean + permittivity[i]
    damping = jnp.full((1, 2 * half), shift[0] * mean * (1.0 / kinds), jnp.float32)
    over_damping = 1.0 / damping
    dz_re, dz_im = difference(3)
    square_z = dz_re**2 + dz_im**2
    square_x = dx[0] ** 2 + dx[1] ** 2
    for k in range(kys):
        dy_re, dy_im = difference(4 + k)
        gain[k] = 1.0 / (square_x + (dy_re**2 + dy_im**2) + square_z + damping)

    (cos_x, sin_x), (cos_y, sin_y), (cos_z, sin_z) = (wave(axis) for axis in range(3))
    cos_up = jnp.where(me == count - 1, cos_x, 1.0)
    sin_up = jnp.where(me == count - 1, sin_x, 0.0)
    cos_dn = jnp.where(me == 0, cos_x, 1.0)
    sin_dn = jnp.where(me == 0, -sin_x, 0.0)
    index_row, low_row = index[0:1], low[0:1]
    last, first = index_row == size - 1, index_row == 0
    zfa = jnp.where(last, jnp.where(low_row, -sin_z, sin_z), 1.0)
    zfb = jnp.where(last, cos_z, 0.0)
    zba = jnp.where(first, jnp.where(low_row, sin_z, -sin_z), 1.0)
    zbb = jnp.where(first, cos_z, 0.0)
    q0, q1 = shift[0], shift[1]

    half_low = low[0 : size // 2]

    def every(x):
        return pl.ds(x, size // 2, stride=planes)

    even, odd = pl.ds(0, size // 2, stride=2), pl.ds(1, size // 2, stride=2)
    for x in range(planes):
        kind = material[every(x), :]
        scaled = jnp.zeros(kind.shape, jnp.float32)
        for i in range(kinds):
            scaled = scaled + jnp.where(kind == i, permittivity[i], jnp.float32(0.0))
        turned = swap(scaled)
        permit[x, even, :] = jnp.where(half_low, scaled, turned)
        permit[x, odd, :] = jnp.where(half_low, turned, scaled)
        for c in range(3):
            re, im = right[0, c, every(x), :], right[1, c, every(x), :]
            res_out[c, x, even, :] = jnp.where(half_low, re, swap(im))
            res_out[c, x, odd, :] = jnp.where(half_low, swap(re), im)

    def emit(flat, field, c, x):
        a, b = field[c, x, even, :], field[c, x, odd, :]
        flat[0, c, every(x), :] = jnp.where(half_low, a, swap(b))
        flat[1, c, every(x), :] = jnp.where(half_low, swap(a), b)

    pl.semaphore_wait(barrier, count - 1)

    permit_copy = copy_to(
        permit.at[planes - 1],
        low_permit,
        halo_send_sem.at[0],
        halo_recv_sem.at[0],
        peer(1),
    )
    permit_copy.start()
    inv_eps[...] = 1.0 / permit[...]

    def halo_copies(it):
        low = copy_to(
            precond.at[it, :, planes - 1],
            low_halo.at[it],
            halo_send_sem.at[1],
            halo_recv_sem.at[1],
            peer(1),
        )
        up = copy_to(
            precond.at[it, 1:3, 0],
            up_halo.at[it],
            halo_send_sem.at[2],
            halo_recv_sem.at[2],
            lax.rem(me + count - 1, count),
        )
        return low, up

    def spectrum_forward(e, c):
        for x in range(planes):
            both = dot(image[c, x], rzf[...])
            mixed = jnp.concatenate([both[:, : 2 * half], both[:, 2 * half :]], 0)
            out = dot(lyf[...], mixed)
            for d in range(count):
                at = d * chunk + x * pad
                send[e, c, at : at + kys, :] = out[d * kys : (d + 1) * kys, :]

    def symbol(k):
        return [(dx[0], dx[1]), difference(4 + k), difference(3)]

    def columns_in(e, c):
        for k in range(kys):
            g = recv[e, c, pl.ds(k, size, stride=pad), :]
            w = dot(lxf[...], jnp.concatenate([g, turn(g)], 0))
            spec[c, k] = w
            re, im = symbol(k)[c]
            term = re * w - im * turn(w)
            if c == 0:
                inner_buf[k] = term
            elif c == 1:
                inner_buf[k] = inner_buf[k] + term
            else:
                inner_buf[k] = (inner_buf[k] + term) * (gain[k] * over_damping)

    def columns_out(e, c):
        for k in range(kys):
            re, im = symbol(k)[c]
            u = spec[c, k] * gain[k] + cmul(re, im, inner_buf[k])
            out = dot(lxi[...], jnp.concatenate([u, turn(u)], 0))
            for d in range(count):
                at = d * chunk + k * pad
                send[e + 1, c, at : at + planes, :] = out[d * planes : (d + 1) * planes, :]

    def field_back(e, c, x):
        v = recv[e + 1, c, pl.ds(x, size, stride=pad), :]
        both = dot(v, rzi[...])
        mixed = jnp.concatenate([both[:, : 2 * half], both[:, 2 * half :]], 0)
        return dot(lyi[...], mixed)

    def next_y(f):
        edge = cmul(cos_y, sin_y, f[0:1])
        return jnp.where(row == size - 1, edge, pltpu.roll(f, size - 1, 0))

    def prev_y(f):
        edge = cmul(cos_y, -sin_y, f[size - 1 : size])
        return jnp.where(row == 0, edge, pltpu.roll(f, 1, 0))

    def next_z(f):
        return pltpu.roll(f, 2 * half - 1, 1) * zfa + pltpu.roll(f, half - 1, 1) * zfb

    def prev_z(f):
        return pltpu.roll(f, 1, 1) * zba + pltpu.roll(f, half + 1, 1) * zbb

    def operate(it):
        for x in range(-1, planes):
            if x < 0:
                e = [cmul(cos_dn, sin_dn, low_halo[it, c]) for c in range(3)]
                inv = inv_low[...]
            else:
                e = [precond[it, c, x] for c in range(3)]
                inv = inv_eps[x]
            if x + 1 < planes:
                up_y, up_z = precond[it, 1, x + 1], precond[it, 2, x + 1]
            else:
                up_y, up_z = (cmul(cos_up, sin_up, up_halo[it, c]) for c in range(2))
            curl_buf[1, x + 1] = ((next_z(e[0]) - e[0]) - (up_z - e[2])) * inv
            curl_buf[2, x + 1] = ((up_y - e[1]) - (next_y(e[0]) - e[0])) * inv
            if x >= 0:
                curl_buf[0, x + 1] = (
                    (next_y(e[2]) - e[2]) - (next_z(e[1]) - e[1])
                ) * inv
        for x in range(planes):
            h = [curl_buf[c, x + 1] for c in range(3)]
            low_y, low_z = curl_buf[1, x], curl_buf[2, x]
            parts = [
                (prev_z(h[1]) - h[1]) - (prev_y(h[2]) - h[2]),
                (low_z - h[2]) - (prev_z(h[0]) - h[0]),
                (prev_y(h[0]) - h[0]) - (low_y - h[1]),
            ]
            for c in range(3):
                operated[c, x] = parts[c] + cmul(q0, q1, precond[it, c, x]) * permit[x]

    def solve(g_re, g_im, s_re, s_im):
        factor = g_im / g_re
        low = (s_im - factor * s_re) / (g_re + factor * g_im)
        return (s_re + g_im * low) / g_re, low

    def folded(value):
        return jnp.sum(value, axis=0, keepdims=True)

    image[...] = res_out[...]
    sol_out[...] = jnp.zeros_like(sol_out)
    direc[...] = jnp.zeros_like(direc)

    def update(coef_re, coef_im):
        for c in range(3):
            for x in range(planes):
                sol_out[c, x] = sol_out[c, x] + cmul(coef_re, coef_im, direc[c, x])
                res_out[c, x] = res_out[c, x] - cmul(coef_re, coef_im, image[c, x])

    def gram_totals(it):
        totals = part_finish(2 * it - 1)
        return totals[0:1], totals[1:2], totals[2:3], totals[3:4]

    def iteration(it, carry):
        e = 2 * it
        for c in range(3):
            spectrum_forward(e, c)
            exchange_start(e, 0, c)
        for c in range(3):
            exchange_finish(e, 0, c)
            columns_in(e, c)
        for c in range(3):
            columns_out(e, c)
            exchange_start(e + 1, 1, c)

        @pl.when(it == 0)
        def _():
            for c in range(3):
                exchange_finish(e + 1, 1, c)
                for x in range(planes):
                    precond[it, c, x] = field_back(e, c, x)
            for copy in halo_copies(it):
                copy.start()
            permit_copy.wait()
            inv_low[...] = 1.0 / low_permit[...]
            for copy in halo_copies(it):
                copy.wait()
            operate(it)
            for c in range(3):
                for x in range(planes):
                    direc[c, x] = precond[it, c, x]
                    image[c, x] = operated[c, x]

        @pl.when(it > 0)
        def _():
            g_re, g_im, s_re, s_im = gram_totals(it)
            coef_re, coef_im = solve(g_re, g_im, s_re, s_im)
            sum_re = jnp.zeros((size, 2 * half), jnp.float32)
            sum_im = jnp.zeros((size, 2 * half), jnp.float32)
            for c in range(3):
                exchange_finish(e + 1, 1, c)
                for x in range(planes):
                    back = field_back(e, c, x)
                    value = precond[it - 1, c, x] - cmul(coef_re, coef_im, back)
                    precond[it, c, x] = value
                    sum_re = sum_re + image[c, x] * value
                    sum_im = sum_im - image[c, x] * turn(value)
            for copy in halo_copies(it):
                copy.start()
            part_send[2 * it, 0:1] = folded(sum_re)
            part_send[2 * it, 1:2] = folded(sum_im)
            part_start(2 * it)
            update(coef_re, coef_im)
            for copy in halo_copies(it):
                copy.wait()
            operate(it)
            totals = part_finish(2 * it)
            beta_re, beta_im = solve(g_re, g_im, totals[0:1], totals[1:2])
            for c in range(3):
                for x in range(planes):
                    direc[c, x] = precond[it, c, x] - cmul(beta_re, beta_im, direc[c, x])
                    image[c, x] = operated[c, x] - cmul(beta_re, beta_im, image[c, x])

        sums = [jnp.zeros((size, 2 * half), jnp.float32) for _ in range(4)]
        for c in range(3):
            for x in range(planes):
                d, m, r = direc[c, x], image[c, x], res_out[c, x]
                td = turn(d)
                sums[0] = sums[0] + d * m
                sums[1] = sums[1] + td * m
                sums[2] = sums[2] + d * r
                sums[3] = sums[3] + td * r
        for i in range(4):
            part_send[2 * it + 1, i : i + 1] = folded(sums[i])
        part_start(2 * it + 1)
        return carry

    part_send[...] = jnp.zeros_like(part_send)
    lax.fori_loop(0, ITERS, iteration, 0)
    update(*solve(*gram_totals(ITERS)))
    for c in range(3):
        for x in range(planes):
            emit(sol_flat, sol_out, c, x)
            emit(res_flat, res_out, c, x)


def on_device(right_side, material, permittivity, bloch_phase, quad_shift):
    planes = right_side.shape[3]
    count = lax.axis_size("px")
    size = planes * count
    lanes = 2 * size
    groups = size // 2
    pad = planes
    while (planes * pad) % 8:
        pad += 1
    f32 = jnp.float32

    def flat(value):
        lead = value.shape[:-2]
        value = value.reshape(lead + (planes, groups, lanes))
        return jnp.swapaxes(value, -3, -2).reshape(lead + (groups * planes, lanes))

    def restored(value):
        value = value.reshape(2, 3, groups, planes, lanes)
        return jnp.swapaxes(value, -3, -2).reshape(right_side.shape)

    vmem = pl.BlockSpec(memory_space=pltpu.VMEM)
    smem = pl.BlockSpec(memory_space=pltpu.SMEM)
    plane = (size, lanes)
    field = pltpu.VMEM((3, planes) + plane, f32)
    planar = pltpu.VMEM((planes,) + plane, f32)
    exchanged = pltpu.VMEM((2 * ITERS, 3, count * planes * pad, lanes), f32)
    dma = pltpu.SemaphoreType.DMA
    out = jax.ShapeDtypeStruct((2, 3, groups * planes, lanes), f32)
    solved, left = pl.pallas_call(
        functools.partial(kernel_body, count, planes, size, pad, permittivity.shape[0]),
        out_shape=(out, out),
        in_specs=[smem] * 3 + [vmem] * 2,
        out_specs=(vmem, vmem),
        scratch_shapes=[
            field,
            field,
            planar,
            pltpu.VMEM((lanes, 2 * lanes), f32),
            pltpu.VMEM(plane, f32),
            pltpu.VMEM(plane, f32),
            pltpu.VMEM((lanes, 2 * lanes), f32),
            pltpu.VMEM(plane, f32),
            pltpu.VMEM(plane, f32),
            pltpu.VMEM((2, -(-(4 + planes) // 8) * 8, lanes), f32),
            pltpu.VMEM((2,) + plane, f32),
            planar,
            field,
            planar,
            exchanged,
            exchanged,
            pltpu.VMEM((ITERS, 3, planes) + plane, f32),
            field,
            field,
            pltpu.VMEM((3, planes + 1) + plane, f32),
            field,
            pltpu.VMEM(plane, f32),
            pltpu.VMEM(plane, f32),
            planar,
            pltpu.VMEM((ITERS, 3) + plane, f32),
            pltpu.VMEM((ITERS, 2) + plane, f32),
            pltpu.VMEM((2 * ITERS, 8, lanes), f32),
            pltpu.VMEM((2 * ITERS, count, 8, lanes), f32),
            dma((2, 3, count)),
            dma((2, 3, count)),
            dma((2, count)),
            dma((2, count)),
            dma((3,)),
            dma((3,)),
        ],
        compiler_params=pltpu.CompilerParams(
            collective_id=0, has_side_effects=True, vmem_limit_bytes=60 * 2**20
        ),
    )(permittivity, bloch_phase, quad_shift, flat(right_side[:, :, 0]), flat(material))
    return restored(solved), restored(left)


def solution(mesh):
    return jax.shard_map(
        on_device,
        mesh=mesh,
        in_specs=(P(None, None, "kpt", "px", None), P("px", None), P(), P("kpt"), P()),
        out_specs=(P(None, None, "kpt", "px", None), P(None, None, "kpt", "px", None)),
        check_vma=False,
    )
```

time: 148 us -> 106 us (0.72)
  other arithmetic: 16 us -> 0 us
  local copies, waits for them, and re-layouts: 17.6 us -> 2.57 us
  Pallas kernels: 108 us -> 103 us
  between operations: 5.32 us -> 0.65 us
    reshape x9 -> x0, local copies, waits for them, and re-layouts: 7.49 us -> none  [the longest x2 2.14 us: restored(): return value.reshape(right_side.shape)]
    pallas_call x1, Pallas kernels: 108 us -> 103 us  [on_device(): pl.pallas_call(functools.partial(kernel_body, count, planes, size, pad, p...]
    concatenate x8 -> x0, other arithmetic: 5.11 us -> none  [the longest x4 2.72 us: left_table(): return jnp.concatenate([table[0], table[1]], 1)]
    add x5 -> x0, other arithmetic: 3.95 us -> none  [the longest x3 1.99 us: on_device(): squares = [re ** 2 + im ** 2 for re, im in diffs]]
    concatenate x1 -> x0, local copies, waits for them, and re-layouts: 3.2 us -> none  [on_device(): jnp.concatenate([jnp.stack([cosines[1], sines[1], jnp.where(is_top, cosin...]
    select_n x5 -> x0, other arithmetic: 2.52 us -> none  [the longest x1 0.68 us: on_device(): jnp.where(last, cosines[2], 0.0)]
    slice x4 -> x0, local copies, waits for them, and re-layouts: 2.48 us -> none  [the longest x1 0.67 us: on_device(): cosines[2]]
    div x5 -> x0, other arithmetic: 2.25 us -> none  [the longest x3 0.83 us: transform_table(): return (jnp.cos(angles).T / size, jnp.sin(angles).T / size)]
where the time goes in v2:
time: 106 us
  Pallas kernels  103 us (97%)
  local copies, waits for them, and re-layouts  2.57 us (2%)
    pallas_call x1, Pallas kernels, on_device(): pl.pallas_call(functools.partial(kernel_body, count, planes, size, pad, p...  103 us
    unnamed x4, local copies, waits for them, and re-layouts  2.57 us

profile of v2, /device:TPU:0, one launch (start us, length us, event | category | flops | bytes accessed | tf_op | source)
XLA Modules:
  0.0 106.2 jit_solution(17303967075918323987)
XLA Ops:
  0.6 103.0 %shard_map.68 = (f32[2,3,128,128]{3,2,1,0:T(8,128)}, f32[2,3,128,128]{3,2,1,0:T(8,128)}) custom-call(f32[3]{0:T(128)} %permittivity.1, f32[3]{0:T(128)} %bloch.1, f32[2]{0:T(128)} %shift.1, f32[2,3,128,128]{3,2,1,0:T(8,128)} %bitcast.22, s32[128,128]{1,0:T(8,128)} %bitcast.23), custom_call_target="tpu_custom_call" | custom-call | tf_op jit(solution)/shard_map/pallas_call | solution.py:512
  103.6 0.0 copy-start
  103.7 1.8 %copy.13 = f32[2,3,1,4,4096]{4,3,2,1,0:T(4,128)} copy(f32[2,3,1,4,4096]{4,3,2,1,0:T(4,128)} %bitcast.21) | data formatting | bytes 786432
  105.5 0.0 copy-done
  105.5 0.7 copy.14
Async XLA Ops:
  103.6 1.8 %copy-start = (f32[2,3,128,128]{3,2,1,0:T(8,128)S(1)}, f32[2,3,128,128]{3,2,1,0:T(8,128)}, u32[]{:S(2)}) copy-start(f32[2,3,128,128]{3,2,1,0:T(8,128)} %get-tuple-element.5) | copy-start | bytes 1179652

commit v3 on v2

--- a/solution.py
+++ b/solution.py
@@ -37,15 +37,19 @@
     permit,
     rzf,
     lyf,
-    lxf,
     rzi,
     lyi,
-    lxi,
     lanes,
-    dx,
-    gain,
+    dy,
+    decay,
+    green,
+    middle,
+    own_decay,
+    wrap,
     spec,
+    solved,
     inner_buf,
+    low_spec,
     send,
     recv,
     precond,
@@ -56,8 +60,6 @@
     low_permit,
     inv_low,
     inv_eps,
-    low_halo,
-    up_halo,
     part_send,
     part_recv,
     a2a_send_sem,
@@ -69,7 +71,7 @@
 ):
     me = lax.axis_index("px")
     kys = size // count
-    chunk = planes * pad
+    chunk = pad
     half = size
 
     def peer(k):
@@ -177,9 +179,7 @@
     def by_cell(axis):
         return jnp.cos(base + bloch[axis] * row.astype(jnp.float32) / size)
 
-    lxf[...] = by_mode(0) * minus_high
     lyf[...] = by_mode(1) * minus_high
-    lxi[...] = by_cell(0) / size
     lyi[...] = by_cell(1) / size
     cells = by_cell(2)
     rzf[0:half, 0 : 2 * half] = cells * minus_high
@@ -192,9 +192,9 @@
     rzi[half:, 0 : 2 * half] = swap(modes) * minus_low
     rzi[half:, 2 * half :] = -modes
 
-    kappa_x = (2.0 * math.pi * row.astype(jnp.float32) + bloch[0]) / size
-    dx[0] = jnp.cos(kappa_x) - 1.0
-    dx[1] = jnp.sin(kappa_x)
+    kappa_y = (2.0 * math.pi * row.astype(jnp.float32) + bloch[1]) / size
+    dy[0] = jnp.cos(kappa_y) - 1.0
+    dy[1] = jnp.sin(kappa_y)
     short = (lanes.shape[1], 2 * half)
     line = lax.broadcasted_iota(jnp.int32, short, 0)
     place = lax.broadcasted_iota(jnp.int32, short, 1)
@@ -202,9 +202,8 @@
     angles = (2.0 * math.pi * place.astype(jnp.float32) + bloch[2]) / size
     for axis in range(3):
         angles = jnp.where(line == axis, bloch[axis], angles)
-    for k in range(kys):
-        ky = (me * kys + k).astype(jnp.float32)
-        angles = jnp.where(line == 4 + k, (2.0 * math.pi * ky + bloch[1]) / size, angles)
+    my_ky = (me * kys + lax.rem(line, kys)).astype(jnp.float32)
+    my_kappa = (2.0 * math.pi * my_ky + bloch[1]) / size
     lanes[0] = jnp.cos(angles)
     lanes[1] = jnp.sin(angles)
 
@@ -220,15 +219,34 @@
     damping = jnp.full((1, 2 * half), shift[0] * mean * (1.0 / kinds), jnp.float32)
     over_damping = 1.0 / damping
     dz_re, dz_im = difference(3)
-    square_z = dz_re**2 + dz_im**2
-    square_x = dx[0] ** 2 + dx[1] ** 2
-    for k in range(kys):
-        dy_re, dy_im = difference(4 + k)
-        gain[k] = 1.0 / (square_x + (dy_re**2 + dy_im**2) + square_z + damping)
-
-    (cos_x, sin_x), (cos_y, sin_y), (cos_z, sin_z) = (wave(axis) for axis in range(3))
-    cos_up = jnp.where(me == count - 1, cos_x, 1.0)
-    sin_up = jnp.where(me == count - 1, sin_x, 0.0)
+    square_z = dz_re**2 + dz_im**2 + damping
+
+    def decay_of(sigma):
+        root = jnp.sqrt(sigma + 0.25 * sigma * sigma)
+        return 1.0 / (1.0 + 0.5 * sigma + root), 0.5 / root
+
+    sigma = dy[0] ** 2 + dy[1] ** 2 + square_z
+    lam, green_value = decay_of(sigma)
+    decay[...] = lam
+    green[...] = green_value
+    middle[...] = 2.0 + sigma
+    my_square = (jnp.cos(my_kappa) - 1.0) ** 2 + jnp.sin(my_kappa) ** 2
+    my_lam, _ = decay_of(my_square + square_z)
+    my_step = my_lam
+    for _ in range(planes - 1):
+        my_step = my_step * my_lam
+    power = jnp.ones(short, jnp.float32)
+    for s in range(count):
+        own_decay[s] = power
+        power = power * my_step
+    own_decay[count] = power
+    is_low = line < kys
+    cos_x, sin_x = wave(0)
+    bottom = 1.0 / (1.0 - 2.0 * power * cos_x + power * power)
+    wrap[0] = (cos_x - power) * bottom
+    wrap[1] = jnp.where(is_low, -sin_x, sin_x) * bottom
+
+    (cos_y, sin_y), (cos_z, sin_z) = wave(1), wave(2)
     cos_dn = jnp.where(me == 0, cos_x, 1.0)
     sin_dn = jnp.where(me == 0, -sin_x, 0.0)
     index_row, low_row = index[0:1], low[0:1]
@@ -275,63 +293,98 @@
     permit_copy.start()
     inv_eps[...] = 1.0 / permit[...]
 
-    def halo_copies(it):
-        low = copy_to(
-            precond.at[it, :, planes - 1],
-            low_halo.at[it],
-            halo_send_sem.at[1],
-            halo_recv_sem.at[1],
+    def plane_copy(it):
+        return copy_to(
+            spec.at[0, planes - 1],
+            low_spec.at[it],
+            halo_send_sem.at[1 + it],
+            halo_recv_sem.at[1 + it],
             peer(1),
         )
-        up = copy_to(
-            precond.at[it, 1:3, 0],
-            up_halo.at[it],
-            halo_send_sem.at[2],
-            halo_recv_sem.at[2],
-            lax.rem(me + count - 1, count),
-        )
-        return low, up
 
     def spectrum_forward(e, c):
+        lam = decay[...]
+        up = down = None
         for x in range(planes):
             both = dot(image[c, x], rzf[...])
             mixed = jnp.concatenate([both[:, : 2 * half], both[:, 2 * half :]], 0)
             out = dot(lyf[...], mixed)
-            for d in range(count):
-                at = d * chunk + x * pad
-                send[e, c, at : at + kys, :] = out[d * kys : (d + 1) * kys, :]
-
-    def symbol(k):
-        return [(dx[0], dx[1]), difference(4 + k), difference(3)]
-
-    def columns_in(e, c):
-        for k in range(kys):
-            g = recv[e, c, pl.ds(k, size, stride=pad), :]
-            w = dot(lxf[...], jnp.concatenate([g, turn(g)], 0))
-            spec[c, k] = w
-            re, im = symbol(k)[c]
-            term = re * w - im * turn(w)
-            if c == 0:
-                inner_buf[k] = term
-            elif c == 1:
-                inner_buf[k] = inner_buf[k] + term
+            spec[c, x] = out
+            if x == 0:
+                up = down = out
+                power = lam
             else:
-                inner_buf[k] = (inner_buf[k] + term) * (gain[k] * over_damping)
-
-    def columns_out(e, c):
-        for k in range(kys):
-            re, im = symbol(k)[c]
-            u = spec[c, k] * gain[k] + cmul(re, im, inner_buf[k])
-            out = dot(lxi[...], jnp.concatenate([u, turn(u)], 0))
-            for d in range(count):
-                at = d * chunk + k * pad
-                send[e + 1, c, at : at + planes, :] = out[d * planes : (d + 1) * planes, :]
-
-    def field_back(e, c, x):
-        v = recv[e + 1, c, pl.ds(x, size, stride=pad), :]
-        both = dot(v, rzi[...])
+                up = up * lam + out
+                down = down + out * power
+                power = power * lam
+        for d in range(count):
+            at = d * chunk
+            send[e, c, at : at + kys, :] = up[d * kys : (d + 1) * kys, :]
+            send[e, c, at + kys : at + 2 * kys, :] = down[d * kys : (d + 1) * kys, :]
+
+    def scan(e, c):
+        step = own_decay[1]
+        below, above = [jnp.zeros(short, jnp.float32)], [jnp.zeros(short, jnp.float32)]
+        for s in range(count):
+            t = count - 1 - s
+            below.append(below[-1] * step + recv[e, c, s * chunk : (s + 1) * chunk, :])
+            above.append(above[-1] * step + recv[e, c, t * chunk : (t + 1) * chunk, :])
+        total = cmul(wrap[0], wrap[1], jnp.where(is_low, below[-1], above[-1]))
+        for d in range(count):
+            t = count - 1 - d
+            value = jnp.where(is_low, below[d], above[t])
+            power = jnp.where(is_low, own_decay[d], own_decay[t])
+            send[e + 1, c, d * chunk : (d + 1) * chunk, :] = value + power * total
+
+    def column_solve(e, c):
+        for s in range(count):
+            at = s * chunk
+            inner_buf[0, s * kys : (s + 1) * kys, :] = recv[e + 1, c, at : at + kys, :]
+            inner_buf[1, s * kys : (s + 1) * kys, :] = recv[
+                e + 1, c, at + kys : at + 2 * kys, :
+            ]
+        lam, scale = decay[...], green[...]
+        total = inner_buf[0]
+        solved[c, 0] = total
+        for x in range(planes):
+            total = total * lam + spec[c, x]
+            solved[c, x + 1] = total
+        total = inner_buf[1]
+        solved[c, planes + 1] = (solved[c, planes] * lam + total) * scale
+        for x in range(planes - 1, -2, -1):
+            total = total * lam
+            solved[c, x + 1] = (solved[c, x + 1] + total) * scale
+            if x >= 0:
+                total = total + spec[c, x]
+
+    def couple(it):
+        dy_re, dy_im = dy[0], dy[1]
+        low = cmul(cos_dn, sin_dn, low_spec[it])
+        prior = middle[...] * solved[0, 0] - solved[0, 1] - low
+        for x in range(planes + 2):
+            here = solved[0, x]
+            term = prior - here
+            prior = here
+            for c, (re, im) in ((1, (dy_re, dy_im)), (2, difference(3))):
+                f = solved[c, x]
+                term = term + re * f - im * turn(f)
+            inner_buf[x] = term * over_damping
+        for x in range(planes + 2):
+            if x <= planes:
+                solved[0, x] = solved[0, x] + (inner_buf[x + 1] - inner_buf[x])
+            inner = inner_buf[x]
+            turned = turn(inner)
+            solved[1, x] = solved[1, x] + dy_re * inner + dy_im * turned
+            dz_re, dz_im = difference(3)
+            solved[2, x] = solved[2, x] + dz_re * inner + dz_im * turned
+
+    def field_back(c, x):
+        both = dot(solved[c, x], rzi[...])
         mixed = jnp.concatenate([both[:, : 2 * half], both[:, 2 * half :]], 0)
         return dot(lyi[...], mixed)
+
+    def wide_planes(c):
+        return planes + (1 if c == 0 else 2)
 
     def next_y(f):
         edge = cmul(cos_y, sin_y, f[0:1])
@@ -347,18 +400,11 @@
     def prev_z(f):
         return pltpu.roll(f, 1, 1) * zba + pltpu.roll(f, half + 1, 1) * zbb
 
-    def operate(it):
+    def operate():
         for x in range(-1, planes):
-            if x < 0:
-                e = [cmul(cos_dn, sin_dn, low_halo[it, c]) for c in range(3)]
-                inv = inv_low[...]
-            else:
-                e = [precond[it, c, x] for c in range(3)]
-                inv = inv_eps[x]
-            if x + 1 < planes:
-                up_y, up_z = precond[it, 1, x + 1], precond[it, 2, x + 1]
-            else:
-                up_y, up_z = (cmul(cos_up, sin_up, up_halo[it, c]) for c in range(2))
+            e = [precond[c, x + 1] for c in range(3)]
+            inv = inv_low[...] if x < 0 else inv_eps[x]
+            up_y, up_z = precond[1, x + 2], precond[2, x + 2]
             curl_buf[1, x + 1] = ((next_z(e[0]) - e[0]) - (up_z - e[2])) * inv
             curl_buf[2, x + 1] = ((up_y - e[1]) - (next_y(e[0]) - e[0])) * inv
             if x >= 0:
@@ -374,7 +420,7 @@
                 (prev_y(h[0]) - h[0]) - (low_y - h[1]),
             ]
             for c in range(3):
-                operated[c, x] = parts[c] + cmul(q0, q1, precond[it, c, x]) * permit[x]
+                operated[c, x] = parts[c] + cmul(q0, q1, precond[c, x + 1]) * permit[x]
 
     def solve(g_re, g_im, s_re, s_im):
         factor = g_im / g_re
@@ -403,29 +449,29 @@
         for c in range(3):
             spectrum_forward(e, c)
             exchange_start(e, 0, c)
+            if c == 0:
+                plane_copy(it).start()
         for c in range(3):
             exchange_finish(e, 0, c)
-            columns_in(e, c)
+            scan(e, c)
+            exchange_start(e + 1, 1, c)
         for c in range(3):
-            columns_out(e, c)
-            exchange_start(e + 1, 1, c)
+            exchange_finish(e + 1, 1, c)
+            column_solve(e, c)
+        plane_copy(it).wait()
+        couple(it)
 
         @pl.when(it == 0)
         def _():
             for c in range(3):
-                exchange_finish(e + 1, 1, c)
-                for x in range(planes):
-                    precond[it, c, x] = field_back(e, c, x)
-            for copy in halo_copies(it):
-                copy.start()
+                for x in range(wide_planes(c)):
+                    precond[c, x] = field_back(c, x)
             permit_copy.wait()
             inv_low[...] = 1.0 / low_permit[...]
-            for copy in halo_copies(it):
-                copy.wait()
-            operate(it)
+            operate()
             for c in range(3):
                 for x in range(planes):
-                    direc[c, x] = precond[it, c, x]
+                    direc[c, x] = precond[c, x + 1]
                     image[c, x] = operated[c, x]
 
         @pl.when(it > 0)
@@ -435,27 +481,22 @@
             sum_re = jnp.zeros((size, 2 * half), jnp.float32)
             sum_im = jnp.zeros((size, 2 * half), jnp.float32)
             for c in range(3):
-                exchange_finish(e + 1, 1, c)
-                for x in range(planes):
-                    back = field_back(e, c, x)
-                    value = precond[it - 1, c, x] - cmul(coef_re, coef_im, back)
-                    precond[it, c, x] = value
-                    sum_re = sum_re + image[c, x] * value
-                    sum_im = sum_im - image[c, x] * turn(value)
-            for copy in halo_copies(it):
-                copy.start()
+                for x in range(wide_planes(c)):
+                    value = precond[c, x] - cmul(coef_re, coef_im, field_back(c, x))
+                    precond[c, x] = value
+                    if 1 <= x <= planes:
+                        sum_re = sum_re + image[c, x - 1] * value
+                        sum_im = sum_im - image[c, x - 1] * turn(value)
             part_send[2 * it, 0:1] = folded(sum_re)
             part_send[2 * it, 1:2] = folded(sum_im)
             part_start(2 * it)
             update(coef_re, coef_im)
-            for copy in halo_copies(it):
-                copy.wait()
-            operate(it)
+            operate()
             totals = part_finish(2 * it)
             beta_re, beta_im = solve(g_re, g_im, totals[0:1], totals[1:2])
             for c in range(3):
                 for x in range(planes):
-                    direc[c, x] = precond[it, c, x] - cmul(beta_re, beta_im, direc[c, x])
+                    direc[c, x] = precond[c, x + 1] - cmul(beta_re, beta_im, direc[c, x])
                     image[c, x] = operated[c, x] - cmul(beta_re, beta_im, image[c, x])
 
         sums = [jnp.zeros((size, 2 * half), jnp.float32) for _ in range(4)]
@@ -487,9 +528,7 @@
     size = planes * count
     lanes = 2 * size
     groups = size // 2
-    pad = planes
-    while (planes * pad) % 8:
-        pad += 1
+    pad = -(-2 * planes // 8) * 8
     f32 = jnp.float32
 
     def flat(value):
@@ -506,7 +545,9 @@
     plane = (size, lanes)
     field = pltpu.VMEM((3, planes) + plane, f32)
     planar = pltpu.VMEM((planes,) + plane, f32)
-    exchanged = pltpu.VMEM((2 * ITERS, 3, count * planes * pad, lanes), f32)
+    exchanged = pltpu.VMEM((2 * ITERS, 3, count * pad, lanes), f32)
+    extended = pltpu.VMEM((3, planes + 2) + plane, f32)
+    rows = (pad, lanes)
     dma = pltpu.SemaphoreType.DMA
     out = jax.ShapeDtypeStruct((2, 3, groups * planes, lanes), f32)
     solved, left = pl.pallas_call(
@@ -520,18 +561,22 @@
             planar,
             pltpu.VMEM((lanes, 2 * lanes), f32),
             pltpu.VMEM(plane, f32),
-            pltpu.VMEM(plane, f32),
             pltpu.VMEM((lanes, 2 * lanes), f32),
             pltpu.VMEM(plane, f32),
+            pltpu.VMEM((2,) + rows, f32),
+            pltpu.VMEM((2,) + plane, f32),
             pltpu.VMEM(plane, f32),
-            pltpu.VMEM((2, -(-(4 + planes) // 8) * 8, lanes), f32),
-            pltpu.VMEM((2,) + plane, f32),
-            planar,
+            pltpu.VMEM(plane, f32),
+            pltpu.VMEM(plane, f32),
+            pltpu.VMEM((count + 1,) + rows, f32),
+            pltpu.VMEM((2,) + rows, f32),
             field,
-            planar,
+            extended,
+            pltpu.VMEM((planes + 2,) + plane, f32),
+            pltpu.VMEM((ITERS,) + plane, f32),
             exchanged,
             exchanged,
-            pltpu.VMEM((ITERS, 3, planes) + plane, f32),
+            extended,
             field,
             field,
             pltpu.VMEM((3, planes + 1) + plane, f32),
@@ -539,16 +584,14 @@
             pltpu.VMEM(plane, f32),
             pltpu.VMEM(plane, f32),
             planar,
-            pltpu.VMEM((ITERS, 3) + plane, f32),
-            pltpu.VMEM((ITERS, 2) + plane, f32),
             pltpu.VMEM((2 * ITERS, 8, lanes), f32),
             pltpu.VMEM((2 * ITERS, count, 8, lanes), f32),
             dma((2, 3, count)),
             dma((2, 3, count)),
             dma((2, count)),
             dma((2, count)),
-            dma((3,)),
-            dma((3,)),
+            dma((1 + ITERS,)),
+            dma((1 + ITERS,)),
         ],
         compiler_params=pltpu.CompilerParams(
             collective_id=0, has_side_effects=True, vmem_limit_bytes=60 * 2**20

time: 106 us -> 74.6 us (0.70)
  Pallas kernels: 103 us -> 71.3 us
    pallas_call x1, Pallas kernels: 103 us -> 71.3 us  [on_device(): pl.pallas_call(functools.partial(kernel_body, count, planes, size, pad, p...]
where the time goes in v3:
time: 74.6 us; the launch traced here: 74.5 us
  Pallas kernels  71.3 us (96%)
  local copies, waits for them, and re-layouts  2.57 us (3%)
    pallas_call x1, Pallas kernels, on_device(): pl.pallas_call(functools.partial(kernel_body, count, planes, size, pad, p...  71.3 us
    unnamed x4, local copies, waits for them, and re-layouts  2.57 us

profile of v3, /device:TPU:0, one launch (start us, length us, event | category | flops | bytes accessed | tf_op | source)
XLA Modules:
  0.0 74.5 jit_solution(18193858035142536174)
XLA Ops:
  0.6 71.3 %shard_map.68 = (f32[2,3,128,128]{3,2,1,0:T(8,128)}, f32[2,3,128,128]{3,2,1,0:T(8,128)}) custom-call(f32[3]{0:T(128)} %permittivity.1, f32[3]{0:T(128)} %bloch.1, f32[2]{0:T(128)} %shift.1, f32[2,3,128,128]{3,2,1,0:T(8,128)} %bitcast.22, s32[128,128]{1,0:T(8,128)} %bitcast.23), custom_call_target="tpu_custom_call" | custom-call | tf_op jit(solution)/shard_map/pallas_call | solution.py:553
  71.9 0.0 copy-start
  71.9 1.8 %copy.13 = f32[2,3,1,4,4096]{4,3,2,1,0:T(4,128)} copy(f32[2,3,1,4,4096]{4,3,2,1,0:T(4,128)} %bitcast.21) | data formatting | bytes 786432
  73.7 0.0 copy-done
  73.7 0.7 %copy.14 = f32[2,3,1,4,4096]{4,3,2,1,0:T(4,128)} copy(f32[2,3,1,4,4096]{4,3,2,1,0:T(4,128)S(1)} %bitcast.20) | data formatting | bytes 786432
Async XLA Ops:
  71.9 1.8 %copy-start = (f32[2,3,128,128]{3,2,1,0:T(8,128)S(1)}, f32[2,3,128,128]{3,2,1,0:T(8,128)}, u32[]{:S(2)}) copy-start(f32[2,3,128,128]{3,2,1,0:T(8,128)} %get-tuple-element.5) | copy-start | bytes 1179652

commit v4 on v3

--- a/solution.py
+++ b/solution.py
@@ -9,7 +9,7 @@
 from jax.sharding import PartitionSpec as P
 
 ITERS = 3
-PRECISE = lax.Precision.HIGHEST
+PRECISE = lax.Precision.HIGH
 MESH = pl.DeviceIdType.MESH
 
 

time: 74.6 us -> 71.6 us (0.960)
  Pallas kernels: 71.3 us -> 68.3 us
    pallas_call x1, Pallas kernels: 71.3 us -> 68.3 us  [on_device(): pl.pallas_call(functools.partial(kernel_body, count, planes, size, pad, p...]
where the time goes in v4:
time: 71.6 us; the launch traced here: 71.5 us
  Pallas kernels  68.3 us (95%)
  local copies, waits for them, and re-layouts  2.57 us (4%)
    pallas_call x1, Pallas kernels, on_device(): pl.pallas_call(functools.partial(kernel_body, count, planes, size, pad, p...  68.3 us
    unnamed x4, local copies, waits for them, and re-layouts  2.57 us

profile of v4, /device:TPU:0, one launch (start us, length us, event | category | flops | bytes accessed | tf_op | source)
XLA Modules:
  0.0 71.5 jit_solution(8796639419362528487)
XLA Ops:
  0.6 68.3 %shard_map.68 = (f32[2,3,128,128]{3,2,1,0:T(8,128)}, f32[2,3,128,128]{3,2,1,0:T(8,128)}) custom-call(f32[3]{0:T(128)} %permittivity.1, f32[3]{0:T(128)} %bloch.1, f32[2]{0:T(128)} %shift.1, f32[2,3,128,128]{3,2,1,0:T(8,128)} %bitcast.22, s32[128,128]{1,0:T(8,128)} %bitcast.23), custom_call_target="tpu_custom_call" | custom-call | tf_op jit(solution)/shard_map/pallas_call | solution.py:553
  68.9 0.0 copy-start
  68.9 1.8 %copy.13 = f32[2,3,1,4,4096]{4,3,2,1,0:T(4,128)} copy(f32[2,3,1,4,4096]{4,3,2,1,0:T(4,128)} %bitcast.21) | data formatting | bytes 786432
  70.7 0.0 copy-done
  70.7 0.7 %copy.14 = f32[2,3,1,4,4096]{4,3,2,1,0:T(4,128)} copy(f32[2,3,1,4,4096]{4,3,2,1,0:T(4,128)S(1)} %bitcast.20) | data formatting | bytes 786432
Async XLA Ops:
  68.9 1.8 %copy-start = (f32[2,3,128,128]{3,2,1,0:T(8,128)S(1)}, f32[2,3,128,128]{3,2,1,0:T(8,128)}, u32[]{:S(2)}) copy-start(f32[2,3,128,128]{3,2,1,0:T(8,128)} %get-tuple-element.5) | copy-start | bytes 1179652
